TPU v7x, 32 devices: a whole 2x2x4 slice. The times are simulated.
32 devices in a mesh: section: 2 (over x), expert: 8 (over z, y), replica: 2 (over core).
Axes of the slice: x: 2, y: 2, z: 4, core: 2. Of those that a mesh axis runs over, the one named last changes fastest.
Arguments:
- token_grads: bfloat16 [2, 512, 3584], P('section', 'expert', 'replica'), may hold values from -6 to 6
- routing: int32 [2, 512, 1], P('section', 'expert'), may hold values from 0 to 1; in each aligned block of 64 rows (0 to 63, 64 to 127, ..., all dimensions but the last counted through in order) at most 34 rows name the same one
- gate_weights: float32 [2, 512, 1], P('section', 'expert'), may hold values from 0.1 to 1
- layer_inputs: bfloat16 [2, 512, 3584], P('section', 'expert', 'replica'), may hold values from -6 to 6
- w_gate: bfloat16 [2, 3584, 2048], P('section', 'replica', 'expert'), may hold values from -0.09375 to 0.09375
- w_up: bfloat16 [2, 3584, 2048], P('section', 'replica', 'expert'), may hold values from -0.09375 to 0.09375
- w_down: bfloat16 [2, 3584, 2048], P('section', 'replica', 'expert'), may hold values from -0.09375 to 0.09375
Outputs:
- upstream: bfloat16 [2, 512, 3584], P('section', 'expert', 'replica')
- grad_gate: bfloat16 [2, 3584, 2048], P('section', 'replica', 'expert')
- grad_up: bfloat16 [2, 3584, 2048], P('section', 'replica', 'expert')
- grad_down: bfloat16 [2, 3584, 2048], P('section', 'replica', 'expert')
Inputs may be any that keep to these rules, and one draw needn't show every extreme that they name: `routing`: each token names 1 different experts. Among the 64 tokens of one group no expert is named more than 34 times, and in every draw some group names some expert exactly 34 times.
All inputs are finite; a program needn't handle non-finite values.
Results may differ from a plain program's by a relative error of at most 0.0064.
Values may be sent and summed in bfloat16 or wider, within the bound.
No kernel may reach another device: no remote copies, remote signals or barrier semaphores. Data moves between devices by JAX's collectives and lax.ppermute only.
A program may use at most 64 MiB of HBM per device.

v0:
```python
import functools

import jax
import jax.numpy as jnp
from jax import lax
from jax.experimental import pallas as pl
from jax.experimental.pallas import tpu as pltpu
from jax.sharding import PartitionSpec as P


SHARES = 4
F32 = jnp.float32
BF16 = jnp.bfloat16
VMEM_BYTES = 16 * 1024 * 1024


def round_up(value, multiple):
    return -(-value // multiple) * multiple


def call(body, out_shape, flops, n_bytes, scratch=(), in_specs=None):
    placed = {} if in_specs is None else {"in_specs": in_specs}
    return functools.partial(
        pl.pallas_call,
        out_shape=out_shape,
        scratch_shapes=list(scratch),
        **placed,
        compiler_params=pltpu.CompilerParams(vmem_limit_bytes=VMEM_BYTES),
        cost_estimate=pl.CostEstimate(flops=flops, bytes_accessed=n_bytes, transcendentals=0),
    )(body)


def in_hbm(value):
    return pltpu.with_memory_space_constraint(value, pltpu.HBM)


def dot(left, right, left_dim=1, right_dim=0):
    return lax.dot_general(
        left, right, (((left_dim,), (right_dim,)), ((), ())), preferred_element_type=F32
    )


def slots(routes, n_experts):
    chosen, n_tokens = routes.shape
    shift = lax.axis_index("expert") // SHARES
    relative = routes - shift
    relative = jnp.where(relative < 0, relative + n_experts, relative)
    experts = lax.broadcasted_iota(jnp.int32, (round_up(n_experts, 8), n_tokens), 0)
    named = [relative[k : k + 1] == experts for k in range(chosen)]
    count = sum(one.astype(F32) for one in named)
    earlier = (
        lax.broadcasted_iota(jnp.int32, (n_tokens, n_tokens), 0)
        < lax.broadcasted_iota(jnp.int32, (n_tokens, n_tokens), 1)
    ).astype(BF16)
    before = dot(count.astype(BF16), earlier)
    slot_rows = []
    for k in range(chosen):
        rank = jnp.sum(jnp.where(named[k], before, 0.0), axis=0, keepdims=True).astype(jnp.int32)
        for other in range(k):
            rank = rank + (relative[other : other + 1] == relative[k : k + 1]).astype(jnp.int32)
        slot_rows.append(rank)
    return relative, slot_rows


def dispatch_blocks(routes, weights, grad_rows, inputs, cuts, capacity):
    n_experts = len(cuts)
    chosen, n_tokens = routes.shape
    columns = inputs.shape[1]
    rows = round_up(2 * capacity, 8)
    order = list(range(1, n_experts)) + [0]

    operands = (routes, weights, inputs, grad_rows)
    first = [sum(len(one) for one in cuts[:which]) for which in range(n_experts)]
    n_outs = first[-1] + len(cuts[-1])

    def body(*refs):
        out_refs = list(refs[len(operands) : len(operands) + n_outs])
        *held, sems = refs[len(operands) + n_outs :]
        routes_ref, weights_ref, inputs_ref, grads_ref = held
        copies = [
            pltpu.make_async_copy(source, target, sems.at[i])
            for i, (source, target) in enumerate(zip(refs, held))
        ]
        for copy in copies:
            copy.start()
        copies[0].wait()
        relative, slot_rows = slots(routes_ref[...], n_experts)
        row = lax.broadcasted_iota(jnp.int32, (rows, n_tokens), 0)
        for copy in copies[1:]:
            copy.wait()
        for which in order:
            pick_input = jnp.zeros((rows, n_tokens), F32)
            pick_grad = jnp.zeros((rows, n_tokens), F32)
            scale = jnp.zeros((rows, n_tokens), F32)
            for k in range(chosen):
                target = jnp.where(relative[k : k + 1] == which, slot_rows[k], -2 * rows)
                pick_input = pick_input + (row == target).astype(F32)
                hit = (row == target + capacity).astype(F32)
                pick_grad = pick_grad + hit
                scale = scale + hit * weights_ref[k : k + 1, :]
            scale = jnp.sum(scale, axis=1, keepdims=True)
            pick_input = pick_input.astype(BF16)
            pick_grad = pick_grad.astype(BF16)
            for part, (begin, end) in enumerate(cuts[which]):
                block = dot(pick_input, inputs_ref[:, begin:end])
                block = block + dot(pick_grad, grads_ref[:, begin:end]) * scale
                out_refs[first[which] + part][...] = block.astype(BF16)

    outs = call(
        body,
        tuple(
            jax.ShapeDtypeStruct((rows, end - begin), BF16) for one in cuts for begin, end in one
        ),
        2 * 2 * n_experts * rows * n_tokens * columns,
        2 * n_tokens * columns * 2 + n_experts * rows * columns * 2,
        [pltpu.VMEM(value.shape, value.dtype) for value in operands]
        + [pltpu.SemaphoreType.DMA((len(operands),))],
        [pl.BlockSpec(memory_space=pltpu.HBM)] * len(operands),
    )(*(in_hbm(value) for value in operands))
    return [
        list(outs[first[which] : first[which] + len(cuts[which])]) for which in range(n_experts)
    ]


def stage_weights(gate_cols, up_cols, down_cols):
    columns, width = gate_cols.shape

    def body(gate_hbm, up_hbm, down_hbm, out_ref, sems):
        copies = [
            pltpu.make_async_copy(ref, out_ref.at[:, i * width : (i + 1) * width], sems.at[i])
            for i, ref in enumerate((gate_hbm, up_hbm, down_hbm))
        ]
        for copy in copies:
            copy.start()
        for copy in copies:
            copy.wait()

    return call(
        body,
        jax.ShapeDtypeStruct((columns, 3 * width), BF16),
        2 * columns * width * 256,
        6 * columns * width * 2,
        [pltpu.SemaphoreType.DMA((3,))],
        [pl.BlockSpec(memory_space=pltpu.HBM)] * 3,
    )(*(in_hbm(value) for value in (gate_cols, up_cols, down_cols)))


def partial_products(blocks, staged, capacity):
    rows = round_up(2 * capacity, 8)
    kept = round_up(capacity, 8)
    n_blocks = len(blocks)
    columns, width = staged.shape[0], staged.shape[1] // 3

    def body(*refs):
        block_refs = list(refs[: sum(len(block) for block in blocks)])
        staged_ref, out_ref, packed_ref = refs[len(block_refs) :]
        for i in range(n_blocks):
            begin = 0
            for _ in blocks[i]:
                ref = block_refs.pop(0)
                end = begin + ref.shape[1]
                packed_ref[i * rows : (i + 1) * rows, begin:end] = ref[...]
                begin = end
        packed = packed_ref[...]
        gate_up = dot(packed, staged_ref[:, : 2 * width])
        down = dot(packed, staged_ref[:, 2 * width :])
        for i in range(n_blocks):
            at = i * rows
            out_ref[i, :, : 2 * width] = gate_up[at : at + kept]
            out_ref[i, :capacity, 2 * width :] = down[at + capacity : at + 2 * capacity]
            if kept > capacity:
                out_ref[i, capacity:, 2 * width :] = jnp.zeros((kept - capacity, width), F32)

    return call(
        body,
        (
            jax.ShapeDtypeStruct((n_blocks, kept, 3 * width), F32),
            jax.ShapeDtypeStruct((n_blocks * rows, columns), BF16),
        ),
        2 * 3 * n_blocks * rows * columns * width,
        3 * columns * width * 2 + n_blocks * rows * columns * 4,
    )(*[part for block in blocks for part in block], staged)


def hidden_backward(partials, staged, capacity, split):
    n_blocks, kept, width3 = partials[0].shape
    columns, width = staged.shape[0], staged.shape[1] // 3
    rows = round_up(2 * capacity, 8)
    n_parts = len(partials)

    def body(*refs):
        part_refs = refs[:n_parts]
        staged_ref = refs[n_parts]
        back_refs = refs[n_parts + 1 : n_parts + 1 + n_blocks]
        slope_ref = refs[n_parts + 1 + n_blocks]
        valid = lax.broadcasted_iota(jnp.int32, (kept, width), 0) < capacity
        d_gates, d_ups = [], []
        slope_ref[...] = jnp.zeros(slope_ref.shape, BF16)
        for i in range(n_blocks):
            total = part_refs[0][i]
            for ref in part_refs[1:]:
                total = total + ref[i]
            gate = jnp.where(valid, total[:, :width], 0.0)
            up = jnp.where(valid, total[:, width : 2 * width], 0.0)
            grad_hidden = total[:, 2 * width :]
            sigmoid_gate = jax.nn.sigmoid(gate)
            activated = gate * sigmoid_gate
            hidden = (activated * up).astype(BF16)
            slope_term = sigmoid_gate * (1.0 + gate * (1.0 - sigmoid_gate))
            d_gate = (grad_hidden * up * slope_term).astype(BF16)
            d_up = (grad_hidden * activated).astype(BF16)
            at = i * rows
            slope_ref[at : at + capacity, :width] = d_gate[:capacity]
            slope_ref[at : at + capacity, width : 2 * width] = d_up[:capacity]
            slope_ref[at + capacity : at + 2 * capacity, 2 * width :] = hidden[:capacity]
            d_gates.append(d_gate)
            d_ups.append(d_up)
        slope = jnp.concatenate(
            [jnp.concatenate(d_gates, axis=0), jnp.concatenate(d_ups, axis=0)], axis=1
        )
        back = dot(slope, staged_ref[:, : 2 * width], 1, 1)
        for i in range(n_blocks):
            part = back[i * kept : i * kept + capacity].astype(BF16)
            back_refs[i][:capacity, :] = part[:, :split]
            back_refs[i][capacity : 2 * capacity, : columns - split] = part[:, split:]
            if columns < 2 * split:
                back_refs[i][capacity : 2 * capacity, columns - split :] = jnp.zeros(
                    (capacity, 2 * split - columns), BF16
                )
            if rows > 2 * capacity:
                back_refs[i][2 * capacity :, :] = jnp.zeros((rows - 2 * capacity, split), BF16)

    outs = call(
        body,
        tuple(jax.ShapeDtypeStruct((rows, split), BF16) for _ in range(n_blocks))
        + (jax.ShapeDtypeStruct((n_blocks * rows, width3), BF16),),
        2 * 2 * n_blocks * kept * columns * width,
        2 * columns * width * 2 + n_blocks * kept * columns * 2,
    )(*partials, staged)
    return outs[:n_blocks], outs[n_blocks]


def weight_grads(packed, slopes, width):
    columns = packed[0].shape[1]
    n_parts = len(packed)
    n_rows = sum(one.shape[0] for one in packed)

    def body(*refs):
        packed_refs = refs[:n_parts]
        slope_refs = refs[n_parts : 2 * n_parts]
        out_refs = refs[2 * n_parts :]
        total = dot(packed_refs[0][...], slope_refs[0][...], 0, 0)
        for left, right in zip(packed_refs[1:], slope_refs[1:]):
            total = total + dot(left[...], right[...], 0, 0)
        for i in range(3):
            out_refs[i][...] = total[:, i * width : (i + 1) * width].astype(BF16)

    return call(
        body,
        tuple(jax.ShapeDtypeStruct((columns, width), BF16) for _ in range(3)),
        2 * 3 * n_rows * columns * width,
        3 * columns * width * 2 + n_rows * columns * 2,
    )(*packed, *slopes)


def combine_near(routes, backs, n_experts, capacity, columns):
    chosen, n_tokens = routes.shape
    rows, split = backs[0].shape
    lanes = round_up(rows, 128)

    def body(routes_ref, *refs):
        back_refs, (base_ref, pick_ref) = refs[:-2], refs[-2:]
        relative, slot_rows = slots(routes_ref[...], n_experts)
        row = lax.broadcasted_iota(jnp.int32, (lanes, n_tokens), 0)
        turned = (
            lax.broadcasted_iota(jnp.int32, (lanes, lanes), 0)
            == lax.broadcasted_iota(jnp.int32, (lanes, lanes), 1)
        ).astype(BF16)
        block = back_refs[0][...].astype(F32)
        for ref in back_refs[1:]:
            block = block + ref[...].astype(F32)
        block = block.astype(BF16)
        for which in range(n_experts):
            for half, (begin, end) in enumerate(((0, split), (split, columns))):
                pick = jnp.zeros((lanes, n_tokens), F32)
                for k in range(chosen):
                    target = jnp.where(relative[k : k + 1] == which, slot_rows[k], -2 * lanes)
                    pick = pick + (row == target + half * capacity).astype(F32)
                pick = dot(pick.astype(BF16), turned, 0, 0).astype(BF16)
                if which:
                    pick_ref[2 * (which - 1) + half] = pick
                else:
                    base_ref[:, begin:end] = dot(pick[:, :rows], block[:, : end - begin])

    return call(
        body,
        (
            jax.ShapeDtypeStruct((n_tokens, columns), F32),
            jax.ShapeDtypeStruct((max(1, 2 * (n_experts - 1)), n_tokens, lanes), BF16),
        ),
        2 * n_tokens * columns * rows,
        rows * columns * 2 * len(backs) + n_tokens * columns * 4,
    )(routes, *backs)


def combine_far(base, picks, merged, columns):
    n_tokens = base.shape[0]
    rows, split = merged[0].shape

    def body(base_ref, pick_ref, *refs):
        merged_refs, out_ref = refs[:-1], refs[-1]
        last = lax.axis_index("section") == lax.axis_size("section") - 1
        for half, (begin, end) in enumerate(((0, split), (split, columns))):
            total = base_ref[:, begin:end]
            for i, ref in enumerate(merged_refs):
                total = total + dot(pick_ref[2 * i + half][:, :rows], ref[:, : end - begin])
            out_ref[:, begin:end] = jnp.where(last, 0.0, total).astype(BF16)

    return call(
        body,
        jax.ShapeDtypeStruct((n_tokens, columns), BF16),
        2 * n_tokens * columns * rows * len(merged),
        rows * columns * 2 * len(merged) + n_tokens * columns * 6,
    )(base, picks, *merged)


def per_device(token_grads, routing, gate_weights, layer_inputs, w_gate, w_up, w_down):
    n_groups = lax.axis_size("expert")
    n_sections = lax.axis_size("section")
    n_replicas = lax.axis_size("replica")
    n_experts = n_groups // SHARES
    grad_rows, inputs = token_grads[0], layer_inputs[0]
    routes, weights = routing[0].T, gate_weights[0].T
    gate_cols, up_cols, down_cols = w_gate[0], w_up[0], w_down[0]
    chosen, n_tokens = routes.shape
    columns = inputs.shape[1]
    width = gate_cols.shape[1]
    capacity = min(n_tokens, 17 * n_tokens * chosen // (16 * n_experts))
    split = round_up(columns // 2, 128)

    def partner(value, step):
        return lax.ppermute(value, "expert", [(j, j ^ step) for j in range(n_groups)])

    def across(j, which):
        expert, share = j // SHARES, j % SHARES
        return (expert + which) % n_experts * SHARES + (share ^ (2 if which else 0))

    def crossing(value, which):
        return lax.ppermute(
            value, "expert", [(j, across(j, which)) for j in range(n_groups)]
        )

    def homeward(value, target):
        pairs = [
            (s * n_groups + j, (s - 1) % n_sections * n_groups + (target(j) if s else j))
            for s in range(n_sections)
            for j in range(n_groups)
        ]
        return lax.ppermute(value, ("section", "expert"), pairs)

    routes_next = lax.ppermute(
        routes, "section", [(s, (s - 1) % n_sections) for s in range(n_sections)]
    )
    lead = max(128, columns * 3 // 7 // 128 * 128)
    halves = ((0, lead), (lead, columns))
    cuts = [((0, columns),)] + [halves] * (n_experts - 1)
    own = dispatch_blocks(routes, weights, grad_rows, inputs, cuts, capacity)
    staged = stage_weights(gate_cols, up_cols, down_cols)
    heads = [own[0]] + [
        [crossing(part, which) for part in own[which]]
        for which in range(1, n_experts)
    ]

    shared = []
    for which, head in enumerate(heads):
        by_y = [partner(part, 1) for part in head]
        by_z = [partner(part, 2) for part in head]
        by_d = [partner(by_z[0], 1)]
        if which:
            by_d.append(partner(by_y[1], 2))
        shared.append((head, by_y, by_z, by_d))

    packed, slopes = [], []

    def returned(blocks):
        part, rows_packed = partial_products(blocks, staged, capacity)
        parts = [part]
        for turn in range(1, n_replicas):
            pairs = [(r, (r + turn) % n_replicas) for r in range(n_replicas)]
            parts.append(lax.ppermute(part, "replica", pairs))
        backs, slope = hidden_backward(parts, staged, capacity, split)
        packed.append(rows_packed)
        slopes.append(slope)
        return list(backs)

    early = SHARES - 1
    chunks = [returned(one[:early]) for one in shared[:2]]
    diagonals = returned([block for one in shared[:2] for block in one[early:]])
    chunks = [chunk + [diagonals[i]] for i, chunk in enumerate(chunks)]
    chunks += [returned(one) for one in shared[2:]]

    near = [homeward(back, lambda j, step=step: j ^ step) for step, back in enumerate(chunks[0])]
    merged = []
    for which in range(1, n_experts):
        backs = chunks[which]
        total = backs[0].astype(F32)
        for step in range(1, SHARES):
            total = total + partner(backs[step], step).astype(F32)
        merged.append(homeward(total.astype(BF16), lambda j, which=which: across(j, -which)))

    base, picks = combine_near(routes_next, near, n_experts, capacity, columns)
    upstream = combine_far(base, picks, merged, columns)
    grad_gate, grad_up, grad_down = weight_grads(packed, slopes, width)
    return (upstream[None], grad_gate[None], grad_up[None], grad_down[None])


def solution(mesh):
    placed = (
        P("section", "expert", "replica"),
        P("section", "expert", None),
        P("section", "expert", None),
        P("section", "expert", "replica"),
        P("section", "replica", "expert"),
        P("section", "replica", "expert"),
        P("section", "replica", "expert"),
    )

    return jax.shard_map(
        per_device,
        mesh=mesh,
        in_specs=placed,
        out_specs=(
            P("section", "expert", "replica"),
            P("section", "replica", "expert"),
            P("section", "replica", "expert"),
            P("section", "replica", "expert"),
        ),
        check_vma=False,
    )
```

profile of v0, /device:TPU:0, one launch (start us, length us, event | category | flops | bytes accessed | tf_op | source)
XLA Modules:
  0.0 63.4 jit_solution(16242491966998191646)
XLA Ops:
  0.6 1.6 %shard_map.102 = (bf16[72,1792]{1,0:T(8,128)(2,1)S(1)}, bf16[72,768]{1,0:T(8,128)(2,1)S(1)}, bf16[72,1024]{1,0:T(8,128)(2,1)S(1)}) custom-call(s32[1,64]{1,0:T(1,128)} %bitcast.18, f32[1,64]{1,0:T(1,128)} %bitcast.17, bf16[64,1792]{1,0:T(8,128)(2,1)} %bitcast.14, bf16[64,1792]{1,0:T(8,128)(2,1)} %bitcast.15), custom_call_target="tpu_custom_call" | custom-call | flops 66060288 | bytes 974848 | tf_op jit(solution)/shard_map/pallas_call | solution.py:109
  2.2 3.1 %collective-permute-start.2 = (bf16[72,1792]{1,0:T(8,128)(2,1)S(1)}, bf16[72,1792]{1,0:T(8,128)(2,1)S(1)}, u32[]{:S(2)}, u32[]{:S(2)}) collective-permute-start(bf16[72,1792]{1,0:T(8,128)(2,1)S(1)} %get-tuple-element.29.refs_0_), channel_id=1, source_target_pairs={{0,4},{2,6},{4,0},{6,2},{8,12},{10,14},{12,8},{14,10},{1,5},{3,7},... | collective-permute-start | bytes 774152 | tf_op jit(solution)/shard_map/ppermute | solution.py:342
  5.3 2.5 %collective-permute-start.8 = (bf16[72,768]{1,0:T(8,128)(2,1)S(1)}, bf16[72,768]{1,0:T(8,128)(2,1)S(1)}, u32[]{:S(2)}, u32[]{:S(2)}) collective-permute-start(bf16[72,768]{1,0:T(8,128)(2,1)S(1)} %get-tuple-element.34), channel_id=1, source_target_pairs={{0,12},{2,14},{4,8},{6,10},{8,4},{10,6},{12,0},{14,2},{1,13},{3,15... | collective-permute-start | bytes 331784 | tf_op jit(solution)/shard_map/ppermute | solution.py:349
  7.8 1.3 %collective-permute-start.11 = (bf16[72,1024]{1,0:T(8,128)(2,1)S(1)}, bf16[72,1024]{1,0:T(8,128)(2,1)S(1)}, u32[]{:S(2)}, u32[]{:S(2)}) collective-permute-start(bf16[72,1024]{1,0:T(8,128)(2,1)S(1)} %get-tuple-element.35), channel_id=1, source_target_pairs={{0,12},{2,14},{4,8},{6,10},{8,4},{10,6},{12,0},{14,2},{1,13},{3,15... | collective-permute-start | bytes 442376 | tf_op jit(solution)/shard_map/ppermute | solution.py:349
  9.1 8.2 %collective-permute-done.8.refs_0_ = bf16[72,768]{1,0:T(8,128)(2,1)S(1)} collective-permute-done((bf16[72,768]{1,0:T(8,128)(2,1)S(1)}, bf16[72,768]{1,0:T(8,128)(2,1)S(1)}, u32[]{:S(2)}, u32[]{:S(2)}) %collective-permute-start.8) | collective-permute-done | bytes 110624 | tf_op jit(solution)/shard_map/ppermute | solution.py:349
  17.3 1.5 %collective-permute-start.16 = (bf16[72,768]{1,0:T(8,128)(2,1)S(1)}, bf16[72,768]{1,0:T(8,128)(2,1)S(1)}, u32[]{:S(2)}, u32[]{:S(2)}) collective-permute-start(bf16[72,768]{1,0:T(8,128)(2,1)S(1)} %collective-permute-done.8.refs_0_), channel_id=1, source_target_pairs={{0,2},{2,0},{4,6},{6,4},{8,10},{10,8},{12,14},{14,12},{1,3},{3,1},... | collective-permute-start | bytes 331784 | tf_op jit(solution)/shard_map/ppermute | solution.py:342
  18.8 0.5 collective-permute-start.1
  19.3 0.0 collective-permute-done.11.refs_1_
  19.4 1.5 %collective-permute-start.12 = (bf16[72,1024]{1,0:T(8,128)(2,1)S(1)}, bf16[72,1024]{1,0:T(8,128)(2,1)S(1)}, u32[]{:S(2)}, u32[]{:S(2)}) collective-permute-start(bf16[72,1024]{1,0:T(8,128)(2,1)S(1)} %collective-permute-done.11.refs_1_), channel_id=1, source_target_pairs={{0,2},{2,0},{4,6},{6,4},{8,10},{10,8},{12,14},{14,12},{1,3},{3,1},... | collective-permute-start | bytes 442376 | tf_op jit(solution)/shard_map/ppermute | solution.py:342
  20.9 0.6 collective-permute-start.17
  21.5 1.8 %collective-permute-done.16.refs_2_ = bf16[72,768]{1,0:T(8,128)(2,1)S(1)} collective-permute-done((bf16[72,768]{1,0:T(8,128)(2,1)S(1)}, bf16[72,768]{1,0:T(8,128)(2,1)S(1)}, u32[]{:S(2)}, u32[]{:S(2)}) %collective-permute-start.16) | collective-permute-done | bytes 110624 | tf_op jit(solution)/shard_map/ppermute | solution.py:342
  23.2 0.0 collective-permute-start.9
  23.3 0.0 collective-permute-done.2.refs_2_
  23.3 1.5 %collective-permute-start.7 = (bf16[72,1792]{1,0:T(8,128)(2,1)S(1)}, bf16[72,1792]{1,0:T(8,128)(2,1)S(1)}, u32[]{:S(2)}, u32[]{:S(2)}) collective-permute-start(bf16[72,1792]{1,0:T(8,128)(2,1)S(1)} %collective-permute-done.2.refs_2_), channel_id=1, source_target_pairs={{0,2},{2,0},{4,6},{6,4},{8,10},{10,8},{12,14},{14,12},{1,3},{3,1},... | collective-permute-start | bytes 774152 | tf_op jit(solution)/shard_map/ppermute | solution.py:342
  24.8 1.8 %shard_map.103.refs_3_.refs_2_.refs_6_ = bf16[1792,768]{1,0:T(8,128)(2,1)S(1)} custom-call(bf16[1792,256]{1,0:T(8,128)(2,1)} %bitcast.11, bf16[1792,256]{1,0:T(8,128)(2,1)} %bitcast.12, bf16[1792,256]{1,0:T(8,128)(2,1)} %bitcast.13), custom_call_target="tpu_custom_call" | custom-call | flops 234881024 | bytes 5505024 | tf_op jit(solution)/shard_map/pallas_call | solution.py:138
  26.5 1.5 %collective-permute-done.9.refs_4_ = bf16[72,768]{1,0:T(8,128)(2,1)S(1)} collective-permute-done((bf16[72,768]{1,0:T(8,128)(2,1)S(1)}, bf16[72,768]{1,0:T(8,128)(2,1)S(1)}, u32[]{:S(2)}, u32[]{:S(2)}) %collective-permute-start.9) | collective-permute-done | bytes 110624 | tf_op jit(solution)/shard_map/ppermute | solution.py:342
  28.0 1.5 %collective-permute-start.10 = (bf16[72,768]{1,0:T(8,128)(2,1)S(1)}, bf16[72,768]{1,0:T(8,128)(2,1)S(1)}, u32[]{:S(2)}, u32[]{:S(2)}) collective-permute-start(bf16[72,768]{1,0:T(8,128)(2,1)S(1)} %collective-permute-done.9.refs_4_), channel_id=1, source_target_pairs={{0,2},{2,0},{4,6},{6,4},{8,10},{10,8},{12,14},{14,12},{1,3},{3,1},... | collective-permute-start | bytes 331784 | tf_op jit(solution)/shard_map/ppermute | solution.py:342
  29.5 2.4 %collective-permute-done.12.refs_3_ = bf16[72,1024]{1,0:T(8,128)(2,1)S(1)} collective-permute-done((bf16[72,1024]{1,0:T(8,128)(2,1)S(1)}, bf16[72,1024]{1,0:T(8,128)(2,1)S(1)}, u32[]{:S(2)}, u32[]{:S(2)}) %collective-permute-start.12) | collective-permute-done | bytes 147488 | tf_op jit(solution)/shard_map/ppermute | solution.py:342
  31.9 0.0 collective-permute-start.13
  31.9 0.0 collective-permute-done.17.refs_5_
  31.9 0.8 %shard_map.109 = (f32[3,40,768]{2,1,0:T(8,128)S(1)}, bf16[216,1792]{1,0:T(8,128)(2,1)S(1)}) custom-call(bf16[72,768]{1,0:T(8,128)(2,1)S(1)} %collective-permute-done.8.refs_0_, bf16[72,1024]{1,0:T(8,128)(2,1)S(1)} %collective-permute-done.11.refs_1_, bf16[72,768]{1,0:T(8,128)(2,1)S(1)} %collective-permute-done.16.refs_2_, ...), custom_call_target="tpu_custom_call" | custom-call | flops 594542592 | bytes 4300800 | tf_op jit(solution)/shard_map/pallas_call | solution.py:174
  32.8 0.1 collective-permute-start.18
  32.8 0.0 collective-permute-done.1.refs_1_
  32.9 0.8 %shard_map.104 = (f32[3,40,768]{2,1,0:T(8,128)S(1)}, bf16[216,1792]{1,0:T(8,128)(2,1)S(1)}) custom-call(bf16[72,1792]{1,0:T(8,128)(2,1)S(1)} %get-tuple-element.29.refs_0_, bf16[72,1792]{1,0:T(8,128)(2,1)S(1)} %collective-permute-done.1.refs_1_, bf16[72,1792]{1,0:T(8,128)(2,1)S(1)} %collective-permute-done.2.refs_2_, ...), custom_call_target="tpu_custom_call" | custom-call | flops 594542592 | bytes 4300800 | tf_op jit(solution)/shard_map/pallas_call | solution.py:174
  33.7 0.5 collective-permute-start.3
  34.2 2.5 %collective-permute-done.10.refs_1_ = bf16[72,768]{1,0:T(8,128)(2,1)S(1)} collective-permute-done((bf16[72,768]{1,0:T(8,128)(2,1)S(1)}, bf16[72,768]{1,0:T(8,128)(2,1)S(1)}, u32[]{:S(2)}, u32[]{:S(2)}) %collective-permute-start.10) | collective-permute-done | bytes 110624 | tf_op jit(solution)/shard_map/ppermute | solution.py:342
  36.7 0.4 collective-permute-done.13.refs_2_
  37.1 0.0 collective-permute-done.7.refs_0_
  37.1 0.6 shard_map.106
  37.7 0.0 copy-start
  37.7 0.1 collective-permute-start.14
  37.8 0.0 collective-permute-done.18.refs_1_
  37.8 0.7 %shard_map.110 = (bf16[72,896]{1,0:T(8,128)(2,1)S(1)}, bf16[72,896]{1,0:T(8,128)(2,1)S(1)}, bf16[72,896]{1,0:T(8,128)(2,1)S(1)}, bf16[216,768]{1,0:T(8,128)(2,1)S(1)}) custom-call(f32[3,40,768]{2,1,0:T(8,128)S(1)} %get-tuple-element.40.refs_0_, f32[3,40,768]{2,1,0:T(8,128)S(1)} %collective-permute-done.18.refs_1_, ...), custom_call_target="tpu_custom_call" | custom-call | flops 220200960 | bytes 2265088 | tf_op jit(solution)/shard_map/pallas_call | solution.py:233
  38.5 1.6 %collective-permute-start.19 = (bf16[72,896]{1,0:T(8,128)(2,1)S(1)}, bf16[72,896]{1,0:T(8,128)(2,1)S(1)}, u32[]{:S(2)}, u32[]{:S(2)}) collective-permute-start(bf16[72,896]{1,0:T(8,128)(2,1)S(1)} %get-tuple-element.42), channel_id=1, source_target_pairs={{0,2},{2,0},{4,6},{6,4},{8,10},{10,8},{12,14},{14,12},{1,3},{3,1},... | collective-permute-start | bytes 387080 | tf_op jit(solution)/shard_map/ppermute | solution.py:342
  40.1 0.0 collective-permute-start.20
  40.1 0.0 collective-permute-done.14.refs_1_
  40.1 0.7 %shard_map.107 = (bf16[72,896]{1,0:T(8,128)(2,1)S(1)}, bf16[72,896]{1,0:T(8,128)(2,1)S(1)}, bf16[144,768]{1,0:T(8,128)(2,1)S(1)}) custom-call(f32[2,40,768]{2,1,0:T(8,128)S(1)} %get-tuple-element.36.refs_0_, f32[2,40,768]{2,1,0:T(8,128)S(1)} %collective-permute-done.14.refs_1_, bf16[1792,768]{1,0:T(8,128)(2,1)S(1)} %shard_map.103.refs_3_.refs_2_.refs_6_), custom_call_target="tpu_custom_call" | custom-call | flops 146800640 | bytes 2121728 | tf_op jit(solution)/shard_map/pallas_call | solution.py:233
  40.8 2.0 %collective-permute-start.21 = (bf16[72,896]{1,0:T(8,128)(2,1)S(1)}, bf16[72,896]{1,0:T(8,128)(2,1)S(1)}, u32[]{:S(2)}, u32[]{:S(2)}) collective-permute-start(bf16[72,896]{1,0:T(8,128)(2,1)S(1)} %get-tuple-element.44), channel_id=1, source_target_pairs={{0,6},{2,4},{4,2},{6,0},{8,14},{10,12},{12,10},{14,8},{1,7},{3,5},... | collective-permute-start | bytes 387080 | tf_op jit(solution)/shard_map/ppermute | solution.py:342
  42.8 0.0 copy-done
  42.8 1.5 %collective-permute-start = (s32[1,64]{1,0:T(1,128)S(1)}, s32[1,64]{1,0:T(1,128)S(1)}, u32[]{:S(2)}, u32[]{:S(2)}) collective-permute-start(s32[1,64]{1,0:T(1,128)S(1)} %bitcast.19), channel_id=1, source_target_pairs={{0,16},{16,0},{1,17},{17,1},{2,18},{18,2},{3,19},{19,3},{4,20},{20... | collective-permute-start | bytes 776 | tf_op jit(solution)/shard_map/ppermute | solution.py:361
  44.3 0.0 collective-permute-done.3.refs_1_
  44.3 0.7 %shard_map.105 = (bf16[72,896]{1,0:T(8,128)(2,1)S(1)}, bf16[72,896]{1,0:T(8,128)(2,1)S(1)}, bf16[72,896]{1,0:T(8,128)(2,1)S(1)}, bf16[216,768]{1,0:T(8,128)(2,1)S(1)}) custom-call(f32[3,40,768]{2,1,0:T(8,128)S(1)} %get-tuple-element.30.refs_0_, f32[3,40,768]{2,1,0:T(8,128)S(1)} %collective-permute-done.3.refs_1_, ...), custom_call_target="tpu_custom_call" | custom-call | flops 220200960 | bytes 2265088 | tf_op jit(solution)/shard_map/pallas_call | solution.py:233
  45.1 0.6 collective-permute-start.4
  45.7 0.0 collective-permute-done.19
  45.7 1.5 %collective-permute-start.5 = (bf16[72,896]{1,0:T(8,128)(2,1)S(1)}, bf16[72,896]{1,0:T(8,128)(2,1)S(1)}, u32[]{:S(2)}, u32[]{:S(2)}) collective-permute-start(bf16[72,896]{1,0:T(8,128)(2,1)S(1)} %get-tuple-element.32), channel_id=1, source_target_pairs={{0,16},{2,18},{4,20},{6,22},{8,24},{10,26},{12,28},{14,30},{16,2},... | collective-permute-start | bytes 387080 | tf_op jit(solution)/shard_map/ppermute | solution.py:359
  47.2 0.0 collective-permute-done.20
  47.2 1.5 %collective-permute-start.6 = (bf16[72,896]{1,0:T(8,128)(2,1)S(1)}, bf16[72,896]{1,0:T(8,128)(2,1)S(1)}, u32[]{:S(2)}, u32[]{:S(2)}) collective-permute-start(bf16[72,896]{1,0:T(8,128)(2,1)S(1)} %get-tuple-element.33), channel_id=1, source_target_pairs={{0,16},{2,18},{4,20},{6,22},{8,24},{10,26},{12,28},{14,30},{16,4},... | collective-permute-start | bytes 387080 | tf_op jit(solution)/shard_map/ppermute | solution.py:359
  48.7 0.0 collective-permute-done.21
  48.7 1.2 %collective-permute-start.15 = (bf16[72,896]{1,0:T(8,128)(2,1)S(1)}, bf16[72,896]{1,0:T(8,128)(2,1)S(1)}, u32[]{:S(2)}, u32[]{:S(2)}) collective-permute-start(bf16[72,896]{1,0:T(8,128)(2,1)S(1)} %get-tuple-element.37), channel_id=1, source_target_pairs={{0,16},{2,18},{4,20},{6,22},{8,24},{10,26},{12,28},{14,30},{16,6},... | collective-permute-start | bytes 387080 | tf_op jit(solution)/shard_map/ppermute | solution.py:359
  49.9 0.1 add_convert_fusion
  49.9 0.0 collective-permute-done.routes_ref
  50.0 1.3 %collective-permute-start.22 = (bf16[72,896]{1,0:T(8,128)(2,1)S(1)}, bf16[72,896]{1,0:T(8,128)(2,1)S(1)}, u32[]{:S(2)}, u32[]{:S(2)}) collective-permute-start(bf16[72,896]{1,0:T(8,128)(2,1)S(1)} %add_convert_fusion), channel_id=1, source_target_pairs={{0,16},{2,18},{4,20},{6,22},{8,24},{10,26},{12,28},{14,30},{16,12}... | collective-permute-start | bytes 387080 | tf_op jit(solution)/shard_map/ppermute | solution.py:359
  51.2 3.6 %shard_map.112 = (bf16[1792,256]{1,0:T(8,128)(2,1)}, bf16[1792,256]{1,0:T(8,128)(2,1)}, bf16[1792,256]{1,0:T(8,128)(2,1)}) custom-call(bf16[216,1792]{1,0:T(8,128)(2,1)S(1)} %get-tuple-element.45.refs_0_, bf16[216,1792]{1,0:T(8,128)(2,1)S(1)} %get-tuple-element.46.refs_1_, bf16[144,1792]{1,0:T(8,128)(2,1)S(1)} %get-tuple-element.47.refs_2_, ...), custom_call_target="tpu_custom_call" | custom-call | flops 1585446912 | bytes 4816896 | tf_op jit(solution)/shard_map/pallas_call | solution.py:258
  54.9 4.7 %collective-permute-done.4.refs_0_ = bf16[72,896]{1,0:T(8,128)(2,1)S(1)} collective-permute-done((bf16[72,896]{1,0:T(8,128)(2,1)S(1)}, bf16[72,896]{1,0:T(8,128)(2,1)S(1)}, u32[]{:S(2)}, u32[]{:S(2)}) %collective-permute-start.4) | collective-permute-done | bytes 129056 | tf_op jit(solution)/shard_map/ppermute | solution.py:359
  59.5 2.3 %collective-permute-done.5.refs_1_ = bf16[72,896]{1,0:T(8,128)(2,1)S(1)} collective-permute-done((bf16[72,896]{1,0:T(8,128)(2,1)S(1)}, bf16[72,896]{1,0:T(8,128)(2,1)S(1)}, u32[]{:S(2)}, u32[]{:S(2)}) %collective-permute-start.5) | collective-permute-done | bytes 129056 | tf_op jit(solution)/shard_map/ppermute | solution.py:359
  61.9 0.0 collective-permute-done.6.refs_2_
  61.9 0.0 collective-permute-done.15.refs_3_
  61.9 0.6 %shard_map.108 = (f32[64,1792]{1,0:T(8,128)S(1)}, bf16[2,64,128]{2,1,0:T(8,128)(2,1)S(1)}) custom-call(s32[1,64]{1,0:T(1,128)S(1)} %collective-permute-done.routes_ref, bf16[72,896]{1,0:T(8,128)(2,1)S(1)} %collective-permute-done.4.refs_0_, bf16[72,896]{1,0:T(8,128)(2,1)S(1)} %collective-permute-done.5.refs_1_, ...), custom_call_target="tpu_custom_call" | custom-call | flops 16515072 | bytes 1490944 | tf_op jit(solution)/shard_map/pallas_call | solution.py:295
  62.6 0.0 collective-permute-done.22.refs_0_
  62.6 0.9 %shard_map.111 = bf16[64,1792]{1,0:T(8,128)(2,1)} custom-call(f32[64,1792]{1,0:T(8,128)S(1)} %get-tuple-element.38.base_ref, bf16[2,64,128]{2,1,0:T(8,128)(2,1)S(1)} %get-tuple-element.39.pick_ref, bf16[72,896]{1,0:T(8,128)(2,1)S(1)} %collective-permute-done.22.refs_0_), custom_call_target="tpu_custom_call" | custom-call | flops 16515072 | bytes 946176 | tf_op jit(solution)/shard_map/pallas_call | solution.py:319
Async XLA Ops:
  2.2 21.1 %collective-permute-start.2 = (bf16[72,1792]{1,0:T(8,128)(2,1)S(1)}, bf16[72,1792]{1,0:T(8,128)(2,1)S(1)}, u32[]{:S(2)}, u32[]{:S(2)}) collective-permute-start(bf16[72,1792]{1,0:T(8,128)(2,1)S(1)} %get-tuple-element.29.refs_0_), channel_id=1, source_target_pairs={{0,4},{2,6},{4,0},{6,2},{8,12},{10,14},{12,8},{14,10},{1,5},{3,7},... | collective-permute-start | bytes 774152 | tf_op jit(solution)/shard_map/ppermute | solution.py:342
  5.3 12.0 %collective-permute-start.8 = (bf16[72,768]{1,0:T(8,128)(2,1)S(1)}, bf16[72,768]{1,0:T(8,128)(2,1)S(1)}, u32[]{:S(2)}, u32[]{:S(2)}) collective-permute-start(bf16[72,768]{1,0:T(8,128)(2,1)S(1)} %get-tuple-element.34), channel_id=1, source_target_pairs={{0,12},{2,14},{4,8},{6,10},{8,4},{10,6},{12,0},{14,2},{1,13},{3,15... | collective-permute-start | bytes 331784 | tf_op jit(solution)/shard_map/ppermute | solution.py:349
  7.8 11.6 %collective-permute-start.11 = (bf16[72,1024]{1,0:T(8,128)(2,1)S(1)}, bf16[72,1024]{1,0:T(8,128)(2,1)S(1)}, u32[]{:S(2)}, u32[]{:S(2)}) collective-permute-start(bf16[72,1024]{1,0:T(8,128)(2,1)S(1)} %get-tuple-element.35), channel_id=1, source_target_pairs={{0,12},{2,14},{4,8},{6,10},{8,4},{10,6},{12,0},{14,2},{1,13},{3,15... | collective-permute-start | bytes 442376 | tf_op jit(solution)/shard_map/ppermute | solution.py:349
  17.3 5.9 %collective-permute-start.16 = (bf16[72,768]{1,0:T(8,128)(2,1)S(1)}, bf16[72,768]{1,0:T(8,128)(2,1)S(1)}, u32[]{:S(2)}, u32[]{:S(2)}) collective-permute-start(bf16[72,768]{1,0:T(8,128)(2,1)S(1)} %collective-permute-done.8.refs_0_), channel_id=1, source_target_pairs={{0,2},{2,0},{4,6},{6,4},{8,10},{10,8},{12,14},{14,12},{1,3},{3,1},... | collective-permute-start | bytes 331784 | tf_op jit(solution)/shard_map/ppermute | solution.py:342
  18.8 14.0 %collective-permute-start.1 = (bf16[72,1792]{1,0:T(8,128)(2,1)S(1)}, bf16[72,1792]{1,0:T(8,128)(2,1)S(1)}, u32[]{:S(2)}, u32[]{:S(2)}) collective-permute-start(bf16[72,1792]{1,0:T(8,128)(2,1)S(1)} %get-tuple-element.29.refs_0_), channel_id=1, source_target_pairs={{0,2},{2,0},{4,6},{6,4},{8,10},{10,8},{12,14},{14,12},{1,3},{3,1},... | collective-permute-start | bytes 774152 | tf_op jit(solution)/shard_map/ppermute | solution.py:342
  19.4 12.6 %collective-permute-start.12 = (bf16[72,1024]{1,0:T(8,128)(2,1)S(1)}, bf16[72,1024]{1,0:T(8,128)(2,1)S(1)}, u32[]{:S(2)}, u32[]{:S(2)}) collective-permute-start(bf16[72,1024]{1,0:T(8,128)(2,1)S(1)} %collective-permute-done.11.refs_1_), channel_id=1, source_target_pairs={{0,2},{2,0},{4,6},{6,4},{8,10},{10,8},{12,14},{14,12},{1,3},{3,1},... | collective-permute-start | bytes 442376 | tf_op jit(solution)/shard_map/ppermute | solution.py:342
  20.9 11.1 %collective-permute-start.17 = (bf16[72,1024]{1,0:T(8,128)(2,1)S(1)}, bf16[72,1024]{1,0:T(8,128)(2,1)S(1)}, u32[]{:S(2)}, u32[]{:S(2)}) collective-permute-start(bf16[72,1024]{1,0:T(8,128)(2,1)S(1)} %collective-permute-done.11.refs_1_), channel_id=1, source_target_pairs={{0,4},{2,6},{4,0},{6,2},{8,12},{10,14},{12,8},{14,10},{1,5},{3,7},... | collective-permute-start | bytes 442376 | tf_op jit(solution)/shard_map/ppermute | solution.py:342
  23.2 4.7 %collective-permute-start.9 = (bf16[72,768]{1,0:T(8,128)(2,1)S(1)}, bf16[72,768]{1,0:T(8,128)(2,1)S(1)}, u32[]{:S(2)}, u32[]{:S(2)}) collective-permute-start(bf16[72,768]{1,0:T(8,128)(2,1)S(1)} %collective-permute-done.8.refs_0_), channel_id=1, source_target_pairs={{0,4},{2,6},{4,0},{6,2},{8,12},{10,14},{12,8},{14,10},{1,5},{3,7},... | collective-permute-start | bytes 331784 | tf_op jit(solution)/shard_map/ppermute | solution.py:342
  23.3 13.8 %collective-permute-start.7 = (bf16[72,1792]{1,0:T(8,128)(2,1)S(1)}, bf16[72,1792]{1,0:T(8,128)(2,1)S(1)}, u32[]{:S(2)}, u32[]{:S(2)}) collective-permute-start(bf16[72,1792]{1,0:T(8,128)(2,1)S(1)} %collective-permute-done.2.refs_2_), channel_id=1, source_target_pairs={{0,2},{2,0},{4,6},{6,4},{8,10},{10,8},{12,14},{14,12},{1,3},{3,1},... | collective-permute-start | bytes 774152 | tf_op jit(solution)/shard_map/ppermute | solution.py:342
  28.0 8.7 %collective-permute-start.10 = (bf16[72,768]{1,0:T(8,128)(2,1)S(1)}, bf16[72,768]{1,0:T(8,128)(2,1)S(1)}, u32[]{:S(2)}, u32[]{:S(2)}) collective-permute-start(bf16[72,768]{1,0:T(8,128)(2,1)S(1)} %collective-permute-done.9.refs_4_), channel_id=1, source_target_pairs={{0,2},{2,0},{4,6},{6,4},{8,10},{10,8},{12,14},{14,12},{1,3},{3,1},... | collective-permute-start | bytes 331784 | tf_op jit(solution)/shard_map/ppermute | solution.py:342
  31.9 5.1 %collective-permute-start.13 = (bf16[72,1024]{1,0:T(8,128)(2,1)S(1)}, bf16[72,1024]{1,0:T(8,128)(2,1)S(1)}, u32[]{:S(2)}, u32[]{:S(2)}) collective-permute-start(bf16[72,1024]{1,0:T(8,128)(2,1)S(1)} %collective-permute-done.12.refs_3_), channel_id=1, source_target_pairs={{0,4},{2,6},{4,0},{6,2},{8,12},{10,14},{12,8},{14,10},{1,5},{3,7},... | collective-permute-start | bytes 442376 | tf_op jit(solution)/shard_map/ppermute | solution.py:342
  32.8 5.0 %collective-permute-start.18 = (f32[3,40,768]{2,1,0:T(8,128)S(1)}, f32[3,40,768]{2,1,0:T(8,128)S(1)}, u32[]{:S(2)}, u32[]{:S(2)}) collective-permute-start(f32[3,40,768]{2,1,0:T(8,128)S(1)} %get-tuple-element.40.refs_0_), channel_id=1, source_target_pairs={{0,1},{1,0},{2,3},{3,2},{4,5},{5,4},{6,7},{7,6},{8,9},{9,8},{10,11... | collective-permute-start | bytes 1105928 | tf_op jit(solution)/shard_map/ppermute | solution.py:390
  33.7 10.7 %collective-permute-start.3 = (f32[3,40,768]{2,1,0:T(8,128)S(1)}, f32[3,40,768]{2,1,0:T(8,128)S(1)}, u32[]{:S(2)}, u32[]{:S(2)}) collective-permute-start(f32[3,40,768]{2,1,0:T(8,128)S(1)} %get-tuple-element.30.refs_0_), channel_id=1, source_target_pairs={{0,1},{1,0},{2,3},{3,2},{4,5},{5,4},{6,7},{7,6},{8,9},{9,8},{10,11... | collective-permute-start | bytes 1105928 | tf_op jit(solution)/shard_map/ppermute | solution.py:390
  37.7 5.2 %copy-start = (s32[1,64,1]{1,2,0:T(1,128)S(1)}, s32[1,64,1]{1,2,0:T(1,128)}, u32[]{:S(2)}) copy-start(s32[1,64,1]{1,2,0:T(1,128)} %param.8) | copy-start | bytes 772
  37.7 2.4 %collective-permute-start.14 = (f32[2,40,768]{2,1,0:T(8,128)S(1)}, f32[2,40,768]{2,1,0:T(8,128)S(1)}, u32[]{:S(2)}, u32[]{:S(2)}) collective-permute-start(f32[2,40,768]{2,1,0:T(8,128)S(1)} %get-tuple-element.36.refs_0_), channel_id=1, source_target_pairs={{0,1},{1,0},{2,3},{3,2},{4,5},{5,4},{6,7},{7,6},{8,9},{9,8},{10,11... | collective-permute-start | bytes 737288 | tf_op jit(solution)/shard_map/ppermute | solution.py:390
  38.5 7.2 %collective-permute-start.19 = (bf16[72,896]{1,0:T(8,128)(2,1)S(1)}, bf16[72,896]{1,0:T(8,128)(2,1)S(1)}, u32[]{:S(2)}, u32[]{:S(2)}) collective-permute-start(bf16[72,896]{1,0:T(8,128)(2,1)S(1)} %get-tuple-element.42), channel_id=1, source_target_pairs={{0,2},{2,0},{4,6},{6,4},{8,10},{10,8},{12,14},{14,12},{1,3},{3,1},... | collective-permute-start | bytes 387080 | tf_op jit(solution)/shard_map/ppermute | solution.py:342
  40.1 7.1 %collective-permute-start.20 = (bf16[72,896]{1,0:T(8,128)(2,1)S(1)}, bf16[72,896]{1,0:T(8,128)(2,1)S(1)}, u32[]{:S(2)}, u32[]{:S(2)}) collective-permute-start(bf16[72,896]{1,0:T(8,128)(2,1)S(1)} %get-tuple-element.43), channel_id=1, source_target_pairs={{0,4},{2,6},{4,0},{6,2},{8,12},{10,14},{12,8},{14,10},{1,5},{3,7},... | collective-permute-start | bytes 387080 | tf_op jit(solution)/shard_map/ppermute | solution.py:342
  40.8 7.9 %collective-permute-start.21 = (bf16[72,896]{1,0:T(8,128)(2,1)S(1)}, bf16[72,896]{1,0:T(8,128)(2,1)S(1)}, u32[]{:S(2)}, u32[]{:S(2)}) collective-permute-start(bf16[72,896]{1,0:T(8,128)(2,1)S(1)} %get-tuple-element.44), channel_id=1, source_target_pairs={{0,6},{2,4},{4,2},{6,0},{8,14},{10,12},{12,10},{14,8},{1,7},{3,5},... | collective-permute-start | bytes 387080 | tf_op jit(solution)/shard_map/ppermute | solution.py:342
  42.8 7.1 %collective-permute-start = (s32[1,64]{1,0:T(1,128)S(1)}, s32[1,64]{1,0:T(1,128)S(1)}, u32[]{:S(2)}, u32[]{:S(2)}) collective-permute-start(s32[1,64]{1,0:T(1,128)S(1)} %bitcast.19), channel_id=1, source_target_pairs={{0,16},{16,0},{1,17},{17,1},{2,18},{18,2},{3,19},{19,3},{4,20},{20... | collective-permute-start | bytes 776 | tf_op jit(solution)/shard_map/ppermute | solution.py:361
  45.1 14.5 %collective-permute-start.4 = (bf16[72,896]{1,0:T(8,128)(2,1)S(1)}, bf16[72,896]{1,0:T(8,128)(2,1)S(1)}, u32[]{:S(2)}, u32[]{:S(2)}) collective-permute-start(bf16[72,896]{1,0:T(8,128)(2,1)S(1)} %get-tuple-element.31), channel_id=1, source_target_pairs={{0,16},{2,18},{4,20},{6,22},{8,24},{10,26},{12,28},{14,30},{16,0},... | collective-permute-start | bytes 387080 | tf_op jit(solution)/shard_map/ppermute | solution.py:359
  45.7 16.2 %collective-permute-start.5 = (bf16[72,896]{1,0:T(8,128)(2,1)S(1)}, bf16[72,896]{1,0:T(8,128)(2,1)S(1)}, u32[]{:S(2)}, u32[]{:S(2)}) collective-permute-start(bf16[72,896]{1,0:T(8,128)(2,1)S(1)} %get-tuple-element.32), channel_id=1, source_target_pairs={{0,16},{2,18},{4,20},{6,22},{8,24},{10,26},{12,28},{14,30},{16,2},... | collective-permute-start | bytes 387080 | tf_op jit(solution)/shard_map/ppermute | solution.py:359
  47.2 14.7 %collective-permute-start.6 = (bf16[72,896]{1,0:T(8,128)(2,1)S(1)}, bf16[72,896]{1,0:T(8,128)(2,1)S(1)}, u32[]{:S(2)}, u32[]{:S(2)}) collective-permute-start(bf16[72,896]{1,0:T(8,128)(2,1)S(1)} %get-tuple-element.33), channel_id=1, source_target_pairs={{0,16},{2,18},{4,20},{6,22},{8,24},{10,26},{12,28},{14,30},{16,4},... | collective-permute-start | bytes 387080 | tf_op jit(solution)/shard_map/ppermute | solution.py:359
  48.7 13.2 %collective-permute-start.15 = (bf16[72,896]{1,0:T(8,128)(2,1)S(1)}, bf16[72,896]{1,0:T(8,128)(2,1)S(1)}, u32[]{:S(2)}, u32[]{:S(2)}) collective-permute-start(bf16[72,896]{1,0:T(8,128)(2,1)S(1)} %get-tuple-element.37), channel_id=1, source_target_pairs={{0,16},{2,18},{4,20},{6,22},{8,24},{10,26},{12,28},{14,30},{16,6},... | collective-permute-start | bytes 387080 | tf_op jit(solution)/shard_map/ppermute | solution.py:359
  50.0 12.6 %collective-permute-start.22 = (bf16[72,896]{1,0:T(8,128)(2,1)S(1)}, bf16[72,896]{1,0:T(8,128)(2,1)S(1)}, u32[]{:S(2)}, u32[]{:S(2)}) collective-permute-start(bf16[72,896]{1,0:T(8,128)(2,1)S(1)} %add_convert_fusion), channel_id=1, source_target_pairs={{0,16},{2,18},{4,20},{6,22},{8,24},{10,26},{12,28},{14,30},{16,12}... | collective-permute-start | bytes 387080 | tf_op jit(solution)/shard_map/ppermute | solution.py:359
where the time goes:
time: 63.6 us; the launch traced here: 63.4 us
  starting transfers between devices  26 us (41%)
  waiting for transfers between devices  23.8 us (37%)
  Pallas kernels  12.8 us (20%)
  between operations  0.78 us (1%)
    ppermute x12, starting transfers between devices, partner(): lax.ppermute(value, 'expert', [(j, j ^ step) for j in range(n_groups)])  13.9 us
    ppermute x12, waiting for transfers between devices, partner(): lax.ppermute(value, 'expert', [(j, j ^ step) for j in range(n_groups)])  8.55 us
    ppermute x2, waiting for transfers between devices, crossing(): lax.ppermute(value, 'expert', [(j, across(j, which)) for j in range(n_gro...  8.2 us
    ppermute x5, waiting for transfers between devices, homeward(): return lax.ppermute(value, ('section', 'expert'), pairs)  7.05 us
    ppermute x5, starting transfers between devices, homeward(): return lax.ppermute(value, ('section', 'expert'), pairs)  6.05 us
    ppermute x2, starting transfers between devices, crossing(): lax.ppermute(value, 'expert', [(j, across(j, which)) for j in range(n_gro...  3.82 us
    pallas_call x1, Pallas kernels, weight_grads(): call(body, tuple((jax.ShapeDtypeStruct((columns, width), BF16) for _ in r...  3.63 us
    pallas_call x3, Pallas kernels, partial_products(): call(body, (jax.ShapeDtypeStruct((n_blocks, kept, 3 * width), F32), jax.S...  2.21 us
  transfers between devices with their start and end apart: 23, of which 8 were waited for; matrix products, arithmetic and copies ran while one was open for 0% of the time, Pallas kernels for 16%

commit v1 on v0

--- a/solution.py
+++ b/solution.py
@@ -18,8 +18,10 @@
     return -(-value // multiple) * multiple
 
 
-def call(body, out_shape, flops, n_bytes, scratch=(), in_specs=None):
+def call(body, out_shape, flops, n_bytes, scratch=(), in_specs=None, out_specs=None):
     placed = {} if in_specs is None else {"in_specs": in_specs}
+    if out_specs is not None:
+        placed["out_specs"] = out_specs
     return functools.partial(
         pl.pallas_call,
         out_shape=out_shape,
@@ -153,7 +155,7 @@
 
     def body(*refs):
         block_refs = list(refs[: sum(len(block) for block in blocks)])
-        staged_ref, out_ref, packed_ref = refs[len(block_refs) :]
+        staged_ref, out_ref, packed_ref, inputs_ref = refs[len(block_refs) :]
         for i in range(n_blocks):
             begin = 0
             for _ in blocks[i]:
@@ -161,12 +163,14 @@
                 end = begin + ref.shape[1]
                 packed_ref[i * rows : (i + 1) * rows, begin:end] = ref[...]
                 begin = end
-        packed = packed_ref[...]
-        gate_up = dot(packed, staged_ref[:, : 2 * width])
-        down = dot(packed, staged_ref[:, 2 * width :])
         for i in range(n_blocks):
             at = i * rows
-            out_ref[i, :, : 2 * width] = gate_up[at : at + kept]
+            inputs_ref[i * kept : (i + 1) * kept] = packed_ref[at : at + kept]
+        gate_up = dot(inputs_ref[...], staged_ref[:, : 2 * width])
+        down = dot(packed_ref[...], staged_ref[:, 2 * width :])
+        for i in range(n_blocks):
+            at = i * rows
+            out_ref[i, :, : 2 * width] = gate_up[i * kept : (i + 1) * kept]
             out_ref[i, :capacity, 2 * width :] = down[at + capacity : at + 2 * capacity]
             if kept > capacity:
                 out_ref[i, capacity:, 2 * width :] = jnp.zeros((kept - capacity, width), F32)
@@ -179,6 +183,7 @@
         ),
         2 * 3 * n_blocks * rows * columns * width,
         3 * columns * width * 2 + n_blocks * rows * columns * 4,
+        [pltpu.VMEM((n_blocks * kept, columns), BF16)],
     )(*[part for block in blocks for part in block], staged)
 
 
@@ -240,7 +245,7 @@
     return outs[:n_blocks], outs[n_blocks]
 
 
-def weight_grads(packed, slopes, width):
+def weight_grads(packed, slopes, width, first, last):
     columns = packed[0].shape[1]
     n_parts = len(packed)
     n_rows = sum(one.shape[0] for one in packed)
@@ -249,17 +254,18 @@
         packed_refs = refs[:n_parts]
         slope_refs = refs[n_parts : 2 * n_parts]
         out_refs = refs[2 * n_parts :]
-        total = dot(packed_refs[0][...], slope_refs[0][...], 0, 0)
+        begin, end = first * width, last * width
+        total = dot(packed_refs[0][...], slope_refs[0][:, begin:end], 0, 0)
         for left, right in zip(packed_refs[1:], slope_refs[1:]):
-            total = total + dot(left[...], right[...], 0, 0)
-        for i in range(3):
+            total = total + dot(left[...], right[:, begin:end], 0, 0)
+        for i in range(last - first):
             out_refs[i][...] = total[:, i * width : (i + 1) * width].astype(BF16)
 
     return call(
         body,
-        tuple(jax.ShapeDtypeStruct((columns, width), BF16) for _ in range(3)),
-        2 * 3 * n_rows * columns * width,
-        3 * columns * width * 2 + n_rows * columns * 2,
+        tuple(jax.ShapeDtypeStruct((columns, width), BF16) for _ in range(last - first)),
+        2 * (last - first) * n_rows * columns * width,
+        (last - first) * columns * width * 2 + n_rows * columns * 2,
     )(*packed, *slopes)
 
 
@@ -308,19 +314,30 @@
     rows, split = merged[0].shape
 
     def body(base_ref, pick_ref, *refs):
-        merged_refs, out_ref = refs[:-1], refs[-1]
+        merged_refs, (out_hbm, held_ref, sems) = refs[:-3], refs[-3:]
         last = lax.axis_index("section") == lax.axis_size("section") - 1
+        copies = []
         for half, (begin, end) in enumerate(((0, split), (split, columns))):
             total = base_ref[:, begin:end]
             for i, ref in enumerate(merged_refs):
                 total = total + dot(pick_ref[2 * i + half][:, :rows], ref[:, : end - begin])
-            out_ref[:, begin:end] = jnp.where(last, 0.0, total).astype(BF16)
+            held_ref[:, begin:end] = jnp.where(last, 0.0, total).astype(BF16)
+            copies.append(
+                pltpu.make_async_copy(
+                    held_ref.at[:, begin:end], out_hbm.at[:, begin:end], sems.at[half]
+                )
+            )
+            copies[-1].start()
+        for copy in copies:
+            copy.wait()
 
     return call(
         body,
         jax.ShapeDtypeStruct((n_tokens, columns), BF16),
         2 * n_tokens * columns * rows * len(merged),
         rows * columns * 2 * len(merged) + n_tokens * columns * 6,
+        [pltpu.VMEM((n_tokens, columns), BF16), pltpu.SemaphoreType.DMA((2,))],
+        out_specs=pl.BlockSpec(memory_space=pltpu.HBM),
     )(base, picks, *merged)
 
 
@@ -410,7 +427,8 @@
 
     base, picks = combine_near(routes_next, near, n_experts, capacity, columns)
     upstream = combine_far(base, picks, merged, columns)
-    grad_gate, grad_up, grad_down = weight_grads(packed, slopes, width)
+    grad_gate, grad_up = weight_grads(packed, slopes, width, 0, 2)
+    (grad_down,) = weight_grads(packed, slopes, width, 2, 3)
     return (upstream[None], grad_gate[None], grad_up[None], grad_down[None])
 
 

time: 63.6 us -> 63.6 us (level)
  Pallas kernels: 12.8 us -> 13.7 us
  waiting for transfers between devices: 23.8 us -> 23 us
    ppermute x5, waiting for transfers between devices: 7.05 us -> 5.91 us  [homeward(): return lax.ppermute(value, ('section', 'expert'), pairs)]
    pallas_call x1 -> x2, Pallas kernels: 3.63 us -> 4.76 us  [weight_grads(): call(body, tuple((jax.ShapeDtypeStruct((columns, width), BF16) for _ in r...]
  transfers between devices with their start and end apart: 23 -> 23, of which waited for: 8 -> 8; matrix products, arithmetic and copies ran while one was open for 0% -> 0% of each run, Pallas kernels for 16% -> 18%
where the time goes in v1:
time: 63.6 us; the launch traced here: 63.5 us
  starting transfers between devices  26 us (41%)
  waiting for transfers between devices  23 us (36%)
  Pallas kernels  13.7 us (22%)
  between operations  0.78 us (1%)
    ppermute x12, starting transfers between devices, partner(): lax.ppermute(value, 'expert', [(j, j ^ step) for j in range(n_groups)])  13.9 us
    ppermute x12, waiting for transfers between devices, partner(): lax.ppermute(value, 'expert', [(j, j ^ step) for j in range(n_groups)])  8.88 us
    ppermute x2, waiting for transfers between devices, crossing(): lax.ppermute(value, 'expert', [(j, across(j, which)) for j in range(n_gro...  8.2 us
    ppermute x5, starting transfers between devices, homeward(): return lax.ppermute(value, ('section', 'expert'), pairs)  6.05 us
    ppermute x5, waiting for transfers between devices, homeward(): return lax.ppermute(value, ('section', 'expert'), pairs)  5.91 us
    pallas_call x2, Pallas kernels, weight_grads(): call(body, tuple((jax.ShapeDtypeStruct((columns, width), BF16) for _ in r...  4.76 us
    ppermute x2, starting transfers between devices, crossing(): lax.ppermute(value, 'expert', [(j, across(j, which)) for j in range(n_gro...  3.82 us
    pallas_call x3, Pallas kernels, hidden_backward(): call(body, tuple((jax.ShapeDtypeStruct((rows, split), BF16) for _ in rang...  2.15 us
  transfers between devices with their start and end apart: 23, of which 8 were waited for; matrix products, arithmetic and copies ran while one was open for 0% of the time, Pallas kernels for 18%

profile of v1, /device:TPU:0, one launch (start us, length us, event | category | flops | bytes accessed | tf_op | source)
XLA Modules:
  0.0 63.5 jit_solution(18053911287086175264)
XLA Ops:
  0.6 1.6 %shard_map.102 = (bf16[72,1792]{1,0:T(8,128)(2,1)S(1)}, bf16[72,768]{1,0:T(8,128)(2,1)S(1)}, bf16[72,1024]{1,0:T(8,128)(2,1)S(1)}) custom-call(s32[1,64]{1,0:T(1,128)} %bitcast.19, f32[1,64]{1,0:T(1,128)} %bitcast.18, bf16[64,1792]{1,0:T(8,128)(2,1)} %bitcast.15, bf16[64,1792]{1,0:T(8,128)(2,1)} %bitcast.16), custom_call_target="tpu_custom_call" | custom-call | flops 66060288 | bytes 974848 | tf_op jit(solution)/shard_map/pallas_call | solution.py:111
  2.2 3.1 %collective-permute-start.2 = (bf16[72,1792]{1,0:T(8,128)(2,1)S(1)}, bf16[72,1792]{1,0:T(8,128)(2,1)S(1)}, u32[]{:S(2)}, u32[]{:S(2)}) collective-permute-start(bf16[72,1792]{1,0:T(8,128)(2,1)S(1)} %get-tuple-element.28.refs_0_), channel_id=1, source_target_pairs={{0,4},{2,6},{4,0},{6,2},{8,12},{10,14},{12,8},{14,10},{1,5},{3,7},... | collective-permute-start | bytes 774152 | tf_op jit(solution)/shard_map/ppermute | solution.py:359
  5.3 2.5 %collective-permute-start.8 = (bf16[72,768]{1,0:T(8,128)(2,1)S(1)}, bf16[72,768]{1,0:T(8,128)(2,1)S(1)}, u32[]{:S(2)}, u32[]{:S(2)}) collective-permute-start(bf16[72,768]{1,0:T(8,128)(2,1)S(1)} %get-tuple-element.33), channel_id=1, source_target_pairs={{0,12},{2,14},{4,8},{6,10},{8,4},{10,6},{12,0},{14,2},{1,13},{3,15... | collective-permute-start | bytes 331784 | tf_op jit(solution)/shard_map/ppermute | solution.py:366
  7.8 1.3 %collective-permute-start.11 = (bf16[72,1024]{1,0:T(8,128)(2,1)S(1)}, bf16[72,1024]{1,0:T(8,128)(2,1)S(1)}, u32[]{:S(2)}, u32[]{:S(2)}) collective-permute-start(bf16[72,1024]{1,0:T(8,128)(2,1)S(1)} %get-tuple-element.34), channel_id=1, source_target_pairs={{0,12},{2,14},{4,8},{6,10},{8,4},{10,6},{12,0},{14,2},{1,13},{3,15... | collective-permute-start | bytes 442376 | tf_op jit(solution)/shard_map/ppermute | solution.py:366
  9.1 8.2 %collective-permute-done.8.refs_0_ = bf16[72,768]{1,0:T(8,128)(2,1)S(1)} collective-permute-done((bf16[72,768]{1,0:T(8,128)(2,1)S(1)}, bf16[72,768]{1,0:T(8,128)(2,1)S(1)}, u32[]{:S(2)}, u32[]{:S(2)}) %collective-permute-start.8) | collective-permute-done | bytes 110624 | tf_op jit(solution)/shard_map/ppermute | solution.py:366
  17.3 1.5 %collective-permute-start.16 = (bf16[72,768]{1,0:T(8,128)(2,1)S(1)}, bf16[72,768]{1,0:T(8,128)(2,1)S(1)}, u32[]{:S(2)}, u32[]{:S(2)}) collective-permute-start(bf16[72,768]{1,0:T(8,128)(2,1)S(1)} %collective-permute-done.8.refs_0_), channel_id=1, source_target_pairs={{0,2},{2,0},{4,6},{6,4},{8,10},{10,8},{12,14},{14,12},{1,3},{3,1},... | collective-permute-start | bytes 331784 | tf_op jit(solution)/shard_map/ppermute | solution.py:359
  18.8 0.5 collective-permute-start.1
  19.3 0.0 collective-permute-done.11.refs_1_
  19.4 1.5 %collective-permute-start.12 = (bf16[72,1024]{1,0:T(8,128)(2,1)S(1)}, bf16[72,1024]{1,0:T(8,128)(2,1)S(1)}, u32[]{:S(2)}, u32[]{:S(2)}) collective-permute-start(bf16[72,1024]{1,0:T(8,128)(2,1)S(1)} %collective-permute-done.11.refs_1_), channel_id=1, source_target_pairs={{0,2},{2,0},{4,6},{6,4},{8,10},{10,8},{12,14},{14,12},{1,3},{3,1},... | collective-permute-start | bytes 442376 | tf_op jit(solution)/shard_map/ppermute | solution.py:359
  20.9 0.6 collective-permute-start.17
  21.5 1.8 %collective-permute-done.16.refs_2_ = bf16[72,768]{1,0:T(8,128)(2,1)S(1)} collective-permute-done((bf16[72,768]{1,0:T(8,128)(2,1)S(1)}, bf16[72,768]{1,0:T(8,128)(2,1)S(1)}, u32[]{:S(2)}, u32[]{:S(2)}) %collective-permute-start.16) | collective-permute-done | bytes 110624 | tf_op jit(solution)/shard_map/ppermute | solution.py:359
  23.2 0.0 collective-permute-start.9
  23.3 0.0 collective-permute-done.2.refs_2_
  23.3 1.5 %collective-permute-start.7 = (bf16[72,1792]{1,0:T(8,128)(2,1)S(1)}, bf16[72,1792]{1,0:T(8,128)(2,1)S(1)}, u32[]{:S(2)}, u32[]{:S(2)}) collective-permute-start(bf16[72,1792]{1,0:T(8,128)(2,1)S(1)} %collective-permute-done.2.refs_2_), channel_id=1, source_target_pairs={{0,2},{2,0},{4,6},{6,4},{8,10},{10,8},{12,14},{14,12},{1,3},{3,1},... | collective-permute-start | bytes 774152 | tf_op jit(solution)/shard_map/ppermute | solution.py:359
  24.8 1.8 %shard_map.103.refs_3_.refs_2_.refs_6_ = bf16[1792,768]{1,0:T(8,128)(2,1)S(1)} custom-call(bf16[1792,256]{1,0:T(8,128)(2,1)} %bitcast.11, bf16[1792,256]{1,0:T(8,128)(2,1)} %bitcast.12, bf16[1792,256]{1,0:T(8,128)(2,1)} %bitcast.13), custom_call_target="tpu_custom_call" | custom-call | flops 234881024 | bytes 5505024 | tf_op jit(solution)/shard_map/pallas_call | solution.py:140
  26.5 1.5 %collective-permute-done.9.refs_4_ = bf16[72,768]{1,0:T(8,128)(2,1)S(1)} collective-permute-done((bf16[72,768]{1,0:T(8,128)(2,1)S(1)}, bf16[72,768]{1,0:T(8,128)(2,1)S(1)}, u32[]{:S(2)}, u32[]{:S(2)}) %collective-permute-start.9) | collective-permute-done | bytes 110624 | tf_op jit(solution)/shard_map/ppermute | solution.py:359
  28.0 1.5 %collective-permute-start.10 = (bf16[72,768]{1,0:T(8,128)(2,1)S(1)}, bf16[72,768]{1,0:T(8,128)(2,1)S(1)}, u32[]{:S(2)}, u32[]{:S(2)}) collective-permute-start(bf16[72,768]{1,0:T(8,128)(2,1)S(1)} %collective-permute-done.9.refs_4_), channel_id=1, source_target_pairs={{0,2},{2,0},{4,6},{6,4},{8,10},{10,8},{12,14},{14,12},{1,3},{3,1},... | collective-permute-start | bytes 331784 | tf_op jit(solution)/shard_map/ppermute | solution.py:359
  29.5 2.4 %collective-permute-done.12.refs_3_ = bf16[72,1024]{1,0:T(8,128)(2,1)S(1)} collective-permute-done((bf16[72,1024]{1,0:T(8,128)(2,1)S(1)}, bf16[72,1024]{1,0:T(8,128)(2,1)S(1)}, u32[]{:S(2)}, u32[]{:S(2)}) %collective-permute-start.12) | collective-permute-done | bytes 147488 | tf_op jit(solution)/shard_map/ppermute | solution.py:359
  31.9 0.0 collective-permute-start.13
  31.9 0.0 collective-permute-done.17.refs_5_
  31.9 0.6 %shard_map.109 = (f32[3,40,768]{2,1,0:T(8,128)S(1)}, bf16[216,1792]{1,0:T(8,128)(2,1)S(1)}) custom-call(bf16[72,768]{1,0:T(8,128)(2,1)S(1)} %collective-permute-done.8.refs_0_, bf16[72,1024]{1,0:T(8,128)(2,1)S(1)} %collective-permute-done.11.refs_1_, bf16[72,768]{1,0:T(8,128)(2,1)S(1)} %collective-permute-done.16.refs_2_, ...), custom_call_target="tpu_custom_call" | custom-call | flops 594542592 | bytes 4300800 | tf_op jit(solution)/shard_map/pallas_call | solution.py:178
  32.6 0.1 collective-permute-start.18
  32.7 0.0 collective-permute-done.1.refs_1_
  32.7 0.6 %shard_map.104 = (f32[3,40,768]{2,1,0:T(8,128)S(1)}, bf16[216,1792]{1,0:T(8,128)(2,1)S(1)}) custom-call(bf16[72,1792]{1,0:T(8,128)(2,1)S(1)} %get-tuple-element.28.refs_0_, bf16[72,1792]{1,0:T(8,128)(2,1)S(1)} %collective-permute-done.1.refs_1_, bf16[72,1792]{1,0:T(8,128)(2,1)S(1)} %collective-permute-done.2.refs_2_, ...), custom_call_target="tpu_custom_call" | custom-call | flops 594542592 | bytes 4300800 | tf_op jit(solution)/shard_map/pallas_call | solution.py:178
  33.3 0.5 collective-permute-start.3
  33.9 2.8 %collective-permute-done.10.refs_1_ = bf16[72,768]{1,0:T(8,128)(2,1)S(1)} collective-permute-done((bf16[72,768]{1,0:T(8,128)(2,1)S(1)}, bf16[72,768]{1,0:T(8,128)(2,1)S(1)}, u32[]{:S(2)}, u32[]{:S(2)}) %collective-permute-start.10) | collective-permute-done | bytes 110624 | tf_op jit(solution)/shard_map/ppermute | solution.py:359
  36.7 0.4 collective-permute-done.13.refs_2_
  37.1 0.0 collective-permute-done.7.refs_0_
  37.1 0.6 shard_map.106
  37.7 0.0 copy-start
  37.7 0.1 collective-permute-start.14
  37.8 0.0 collective-permute-done.18.refs_1_
  37.8 0.7 %shard_map.110 = (bf16[72,896]{1,0:T(8,128)(2,1)S(1)}, bf16[72,896]{1,0:T(8,128)(2,1)S(1)}, bf16[72,896]{1,0:T(8,128)(2,1)S(1)}, bf16[216,768]{1,0:T(8,128)(2,1)S(1)}) custom-call(f32[3,40,768]{2,1,0:T(8,128)S(1)} %get-tuple-element.39.refs_0_, f32[3,40,768]{2,1,0:T(8,128)S(1)} %collective-permute-done.18.refs_1_, ...), custom_call_target="tpu_custom_call" | custom-call | flops 220200960 | bytes 2265088 | tf_op jit(solution)/shard_map/pallas_call | solution.py:238
  38.6 1.6 %collective-permute-start.19 = (bf16[72,896]{1,0:T(8,128)(2,1)S(1)}, bf16[72,896]{1,0:T(8,128)(2,1)S(1)}, u32[]{:S(2)}, u32[]{:S(2)}) collective-permute-start(bf16[72,896]{1,0:T(8,128)(2,1)S(1)} %get-tuple-element.41), channel_id=1, source_target_pairs={{0,2},{2,0},{4,6},{6,4},{8,10},{10,8},{12,14},{14,12},{1,3},{3,1},... | collective-permute-start | bytes 387080 | tf_op jit(solution)/shard_map/ppermute | solution.py:359
  40.1 0.0 collective-permute-start.20
  40.2 0.0 collective-permute-done.14.refs_1_
  40.2 0.7 %shard_map.107 = (bf16[72,896]{1,0:T(8,128)(2,1)S(1)}, bf16[72,896]{1,0:T(8,128)(2,1)S(1)}, bf16[144,768]{1,0:T(8,128)(2,1)S(1)}) custom-call(f32[2,40,768]{2,1,0:T(8,128)S(1)} %get-tuple-element.35.refs_0_, f32[2,40,768]{2,1,0:T(8,128)S(1)} %collective-permute-done.14.refs_1_, bf16[1792,768]{1,0:T(8,128)(2,1)S(1)} %shard_map.103.refs_3_.refs_2_.refs_6_), custom_call_target="tpu_custom_call" | custom-call | flops 146800640 | bytes 2121728 | tf_op jit(solution)/shard_map/pallas_call | solution.py:238
  40.9 2.0 %collective-permute-start.21 = (bf16[72,896]{1,0:T(8,128)(2,1)S(1)}, bf16[72,896]{1,0:T(8,128)(2,1)S(1)}, u32[]{:S(2)}, u32[]{:S(2)}) collective-permute-start(bf16[72,896]{1,0:T(8,128)(2,1)S(1)} %get-tuple-element.43), channel_id=1, source_target_pairs={{0,6},{2,4},{4,2},{6,0},{8,14},{10,12},{12,10},{14,8},{1,7},{3,5},... | collective-permute-start | bytes 387080 | tf_op jit(solution)/shard_map/ppermute | solution.py:359
  42.9 0.0 copy-done
  42.9 1.5 %collective-permute-start = (s32[1,64]{1,0:T(1,128)S(1)}, s32[1,64]{1,0:T(1,128)S(1)}, u32[]{:S(2)}, u32[]{:S(2)}) collective-permute-start(s32[1,64]{1,0:T(1,128)S(1)} %bitcast.20), channel_id=1, source_target_pairs={{0,16},{16,0},{1,17},{17,1},{2,18},{18,2},{3,19},{19,3},{4,20},{20... | collective-permute-start | bytes 776 | tf_op jit(solution)/shard_map/ppermute | solution.py:378
  44.4 0.0 collective-permute-done.3.refs_1_
  44.4 0.7 %shard_map.105 = (bf16[72,896]{1,0:T(8,128)(2,1)S(1)}, bf16[72,896]{1,0:T(8,128)(2,1)S(1)}, bf16[72,896]{1,0:T(8,128)(2,1)S(1)}, bf16[216,768]{1,0:T(8,128)(2,1)S(1)}) custom-call(f32[3,40,768]{2,1,0:T(8,128)S(1)} %get-tuple-element.29.refs_0_, f32[3,40,768]{2,1,0:T(8,128)S(1)} %collective-permute-done.3.refs_1_, ...), custom_call_target="tpu_custom_call" | custom-call | flops 220200960 | bytes 2265088 | tf_op jit(solution)/shard_map/pallas_call | solution.py:238
  45.1 0.6 collective-permute-start.4
  45.7 0.0 collective-permute-done.19
  45.7 1.5 %collective-permute-start.5 = (bf16[72,896]{1,0:T(8,128)(2,1)S(1)}, bf16[72,896]{1,0:T(8,128)(2,1)S(1)}, u32[]{:S(2)}, u32[]{:S(2)}) collective-permute-start(bf16[72,896]{1,0:T(8,128)(2,1)S(1)} %get-tuple-element.31), channel_id=1, source_target_pairs={{0,16},{2,18},{4,20},{6,22},{8,24},{10,26},{12,28},{14,30},{16,2},... | collective-permute-start | bytes 387080 | tf_op jit(solution)/shard_map/ppermute | solution.py:376
  47.2 0.0 collective-permute-done.20
  47.2 1.5 %collective-permute-start.6 = (bf16[72,896]{1,0:T(8,128)(2,1)S(1)}, bf16[72,896]{1,0:T(8,128)(2,1)S(1)}, u32[]{:S(2)}, u32[]{:S(2)}) collective-permute-start(bf16[72,896]{1,0:T(8,128)(2,1)S(1)} %get-tuple-element.32), channel_id=1, source_target_pairs={{0,16},{2,18},{4,20},{6,22},{8,24},{10,26},{12,28},{14,30},{16,4},... | collective-permute-start | bytes 387080 | tf_op jit(solution)/shard_map/ppermute | solution.py:376
  48.7 0.0 collective-permute-done.21
  48.7 1.2 %collective-permute-start.15 = (bf16[72,896]{1,0:T(8,128)(2,1)S(1)}, bf16[72,896]{1,0:T(8,128)(2,1)S(1)}, u32[]{:S(2)}, u32[]{:S(2)}) collective-permute-start(bf16[72,896]{1,0:T(8,128)(2,1)S(1)} %get-tuple-element.36), channel_id=1, source_target_pairs={{0,16},{2,18},{4,20},{6,22},{8,24},{10,26},{12,28},{14,30},{16,6},... | collective-permute-start | bytes 387080 | tf_op jit(solution)/shard_map/ppermute | solution.py:376
  49.9 0.1 add_convert_fusion
  50.0 0.0 collective-permute-done.routes_ref
  50.0 1.3 %collective-permute-start.22 = (bf16[72,896]{1,0:T(8,128)(2,1)S(1)}, bf16[72,896]{1,0:T(8,128)(2,1)S(1)}, u32[]{:S(2)}, u32[]{:S(2)}) collective-permute-start(bf16[72,896]{1,0:T(8,128)(2,1)S(1)} %add_convert_fusion), channel_id=1, source_target_pairs={{0,16},{2,18},{4,20},{6,22},{8,24},{10,26},{12,28},{14,30},{16,12}... | collective-permute-start | bytes 387080 | tf_op jit(solution)/shard_map/ppermute | solution.py:376
  51.3 1.9 %shard_map.113 = bf16[1792,256]{1,0:T(8,128)(2,1)} custom-call(bf16[216,1792]{1,0:T(8,128)(2,1)S(1)} %get-tuple-element.44.refs_0_, bf16[216,1792]{1,0:T(8,128)(2,1)S(1)} %get-tuple-element.45.refs_1_, bf16[144,1792]{1,0:T(8,128)(2,1)S(1)} %get-tuple-element.46.refs_2_, bf16[216,768]{1,0:T(8,128)(2,1)S(1)} %get-tuple-element.47.refs_3_, ...), custom_call_target="tpu_custom_call" | custom-call | flops 528482304 | bytes 2981888 | tf_op jit(solution)/shard_map/pallas_call | solution.py:264
  53.1 2.9 %shard_map.112 = (bf16[1792,256]{1,0:T(8,128)(2,1)}, bf16[1792,256]{1,0:T(8,128)(2,1)}) custom-call(bf16[216,1792]{1,0:T(8,128)(2,1)S(1)} %get-tuple-element.44.refs_0_, bf16[216,1792]{1,0:T(8,128)(2,1)S(1)} %get-tuple-element.45.refs_1_, bf16[144,1792]{1,0:T(8,128)(2,1)S(1)} %get-tuple-element.46.refs_2_, bf16[216,768]{1,0:T(8,128)(2,1)S(1)} %get-tuple-element.47.refs_3_, ...), custom_call_target="tpu_custom_call" | custom-call | flops 1056964608 | bytes 3899392 | tf_op jit(solution)/shard_map/pallas_call | solution.py:264
  56.0 3.6 %collective-permute-done.4.refs_0_ = bf16[72,896]{1,0:T(8,128)(2,1)S(1)} collective-permute-done((bf16[72,896]{1,0:T(8,128)(2,1)S(1)}, bf16[72,896]{1,0:T(8,128)(2,1)S(1)}, u32[]{:S(2)}, u32[]{:S(2)}) %collective-permute-start.4) | collective-permute-done | bytes 129056 | tf_op jit(solution)/shard_map/ppermute | solution.py:376
  59.6 2.3 %collective-permute-done.5.refs_1_ = bf16[72,896]{1,0:T(8,128)(2,1)S(1)} collective-permute-done((bf16[72,896]{1,0:T(8,128)(2,1)S(1)}, bf16[72,896]{1,0:T(8,128)(2,1)S(1)}, u32[]{:S(2)}, u32[]{:S(2)}) %collective-permute-start.5) | collective-permute-done | bytes 129056 | tf_op jit(solution)/shard_map/ppermute | solution.py:376
  61.9 0.0 collective-permute-done.6.refs_2_
  61.9 0.0 collective-permute-done.15.refs_3_
  61.9 0.6 %shard_map.108 = (f32[64,1792]{1,0:T(8,128)S(1)}, bf16[2,64,128]{2,1,0:T(8,128)(2,1)S(1)}) custom-call(s32[1,64]{1,0:T(1,128)S(1)} %collective-permute-done.routes_ref, bf16[72,896]{1,0:T(8,128)(2,1)S(1)} %collective-permute-done.4.refs_0_, bf16[72,896]{1,0:T(8,128)(2,1)S(1)} %collective-permute-done.5.refs_1_, ...), custom_call_target="tpu_custom_call" | custom-call | flops 16515072 | bytes 1490944 | tf_op jit(solution)/shard_map/pallas_call | solution.py:301
  62.6 0.0 collective-permute-done.22.refs_0_
  62.6 0.9 %shard_map.111 = bf16[64,1792]{1,0:T(8,128)(2,1)} custom-call(f32[64,1792]{1,0:T(8,128)S(1)} %get-tuple-element.37.base_ref, bf16[2,64,128]{2,1,0:T(8,128)(2,1)S(1)} %get-tuple-element.38.pick_ref, bf16[72,896]{1,0:T(8,128)(2,1)S(1)} %collective-permute-done.22.refs_0_), custom_call_target="tpu_custom_call" | custom-call | flops 16515072 | bytes 946176 | tf_op jit(solution)/shard_map/pallas_call | solution.py:334
Async XLA Ops:
  2.2 21.1 %collective-permute-start.2 = (bf16[72,1792]{1,0:T(8,128)(2,1)S(1)}, bf16[72,1792]{1,0:T(8,128)(2,1)S(1)}, u32[]{:S(2)}, u32[]{:S(2)}) collective-permute-start(bf16[72,1792]{1,0:T(8,128)(2,1)S(1)} %get-tuple-element.28.refs_0_), channel_id=1, source_target_pairs={{0,4},{2,6},{4,0},{6,2},{8,12},{10,14},{12,8},{14,10},{1,5},{3,7},... | collective-permute-start | bytes 774152 | tf_op jit(solution)/shard_map/ppermute | solution.py:359
  5.3 12.0 %collective-permute-start.8 = (bf16[72,768]{1,0:T(8,128)(2,1)S(1)}, bf16[72,768]{1,0:T(8,128)(2,1)S(1)}, u32[]{:S(2)}, u32[]{:S(2)}) collective-permute-start(bf16[72,768]{1,0:T(8,128)(2,1)S(1)} %get-tuple-element.33), channel_id=1, source_target_pairs={{0,12},{2,14},{4,8},{6,10},{8,4},{10,6},{12,0},{14,2},{1,13},{3,15... | collective-permute-start | bytes 331784 | tf_op jit(solution)/shard_map/ppermute | solution.py:366
  7.8 11.6 %collective-permute-start.11 = (bf16[72,1024]{1,0:T(8,128)(2,1)S(1)}, bf16[72,1024]{1,0:T(8,128)(2,1)S(1)}, u32[]{:S(2)}, u32[]{:S(2)}) collective-permute-start(bf16[72,1024]{1,0:T(8,128)(2,1)S(1)} %get-tuple-element.34), channel_id=1, source_target_pairs={{0,12},{2,14},{4,8},{6,10},{8,4},{10,6},{12,0},{14,2},{1,13},{3,15... | collective-permute-start | bytes 442376 | tf_op jit(solution)/shard_map/ppermute | solution.py:366
  17.3 5.9 %collective-permute-start.16 = (bf16[72,768]{1,0:T(8,128)(2,1)S(1)}, bf16[72,768]{1,0:T(8,128)(2,1)S(1)}, u32[]{:S(2)}, u32[]{:S(2)}) collective-permute-start(bf16[72,768]{1,0:T(8,128)(2,1)S(1)} %collective-permute-done.8.refs_0_), channel_id=1, source_target_pairs={{0,2},{2,0},{4,6},{6,4},{8,10},{10,8},{12,14},{14,12},{1,3},{3,1},... | collective-permute-start | bytes 331784 | tf_op jit(solution)/shard_map/ppermute | solution.py:359
  18.8 13.8 %collective-permute-start.1 = (bf16[72,1792]{1,0:T(8,128)(2,1)S(1)}, bf16[72,1792]{1,0:T(8,128)(2,1)S(1)}, u32[]{:S(2)}, u32[]{:S(2)}) collective-permute-start(bf16[72,1792]{1,0:T(8,128)(2,1)S(1)} %get-tuple-element.28.refs_0_), channel_id=1, source_target_pairs={{0,2},{2,0},{4,6},{6,4},{8,10},{10,8},{12,14},{14,12},{1,3},{3,1},... | collective-permute-start | bytes 774152 | tf_op jit(solution)/shard_map/ppermute | solution.py:359
  19.4 12.6 %collective-permute-start.12 = (bf16[72,1024]{1,0:T(8,128)(2,1)S(1)}, bf16[72,1024]{1,0:T(8,128)(2,1)S(1)}, u32[]{:S(2)}, u32[]{:S(2)}) collective-permute-start(bf16[72,1024]{1,0:T(8,128)(2,1)S(1)} %collective-permute-done.11.refs_1_), channel_id=1, source_target_pairs={{0,2},{2,0},{4,6},{6,4},{8,10},{10,8},{12,14},{14,12},{1,3},{3,1},... | collective-permute-start | bytes 442376 | tf_op jit(solution)/shard_map/ppermute | solution.py:359
  20.9 11.1 %collective-permute-start.17 = (bf16[72,1024]{1,0:T(8,128)(2,1)S(1)}, bf16[72,1024]{1,0:T(8,128)(2,1)S(1)}, u32[]{:S(2)}, u32[]{:S(2)}) collective-permute-start(bf16[72,1024]{1,0:T(8,128)(2,1)S(1)} %collective-permute-done.11.refs_1_), channel_id=1, source_target_pairs={{0,4},{2,6},{4,0},{6,2},{8,12},{10,14},{12,8},{14,10},{1,5},{3,7},... | collective-permute-start | bytes 442376 | tf_op jit(solution)/shard_map/ppermute | solution.py:359
  23.2 4.7 %collective-permute-start.9 = (bf16[72,768]{1,0:T(8,128)(2,1)S(1)}, bf16[72,768]{1,0:T(8,128)(2,1)S(1)}, u32[]{:S(2)}, u32[]{:S(2)}) collective-permute-start(bf16[72,768]{1,0:T(8,128)(2,1)S(1)} %collective-permute-done.8.refs_0_), channel_id=1, source_target_pairs={{0,4},{2,6},{4,0},{6,2},{8,12},{10,14},{12,8},{14,10},{1,5},{3,7},... | collective-permute-start | bytes 331784 | tf_op jit(solution)/shard_map/ppermute | solution.py:359
  23.3 13.8 %collective-permute-start.7 = (bf16[72,1792]{1,0:T(8,128)(2,1)S(1)}, bf16[72,1792]{1,0:T(8,128)(2,1)S(1)}, u32[]{:S(2)}, u32[]{:S(2)}) collective-permute-start(bf16[72,1792]{1,0:T(8,128)(2,1)S(1)} %collective-permute-done.2.refs_2_), channel_id=1, source_target_pairs={{0,2},{2,0},{4,6},{6,4},{8,10},{10,8},{12,14},{14,12},{1,3},{3,1},... | collective-permute-start | bytes 774152 | tf_op jit(solution)/shard_map/ppermute | solution.py:359
  28.0 8.7 %collective-permute-start.10 = (bf16[72,768]{1,0:T(8,128)(2,1)S(1)}, bf16[72,768]{1,0:T(8,128)(2,1)S(1)}, u32[]{:S(2)}, u32[]{:S(2)}) collective-permute-start(bf16[72,768]{1,0:T(8,128)(2,1)S(1)} %collective-permute-done.9.refs_4_), channel_id=1, source_target_pairs={{0,2},{2,0},{4,6},{6,4},{8,10},{10,8},{12,14},{14,12},{1,3},{3,1},... | collective-permute-start | bytes 331784 | tf_op jit(solution)/shard_map/ppermute | solution.py:359
  31.9 5.1 %collective-permute-start.13 = (bf16[72,1024]{1,0:T(8,128)(2,1)S(1)}, bf16[72,1024]{1,0:T(8,128)(2,1)S(1)}, u32[]{:S(2)}, u32[]{:S(2)}) collective-permute-start(bf16[72,1024]{1,0:T(8,128)(2,1)S(1)} %collective-permute-done.12.refs_3_), channel_id=1, source_target_pairs={{0,4},{2,6},{4,0},{6,2},{8,12},{10,14},{12,8},{14,10},{1,5},{3,7},... | collective-permute-start | bytes 442376 | tf_op jit(solution)/shard_map/ppermute | solution.py:359
  32.6 5.2 %collective-permute-start.18 = (f32[3,40,768]{2,1,0:T(8,128)S(1)}, f32[3,40,768]{2,1,0:T(8,128)S(1)}, u32[]{:S(2)}, u32[]{:S(2)}) collective-permute-start(f32[3,40,768]{2,1,0:T(8,128)S(1)} %get-tuple-element.39.refs_0_), channel_id=1, source_target_pairs={{0,1},{1,0},{2,3},{3,2},{4,5},{5,4},{6,7},{7,6},{8,9},{9,8},{10,11... | collective-permute-start | bytes 1105928 | tf_op jit(solution)/shard_map/ppermute | solution.py:407
  33.3 11.0 %collective-permute-start.3 = (f32[3,40,768]{2,1,0:T(8,128)S(1)}, f32[3,40,768]{2,1,0:T(8,128)S(1)}, u32[]{:S(2)}, u32[]{:S(2)}) collective-permute-start(f32[3,40,768]{2,1,0:T(8,128)S(1)} %get-tuple-element.29.refs_0_), channel_id=1, source_target_pairs={{0,1},{1,0},{2,3},{3,2},{4,5},{5,4},{6,7},{7,6},{8,9},{9,8},{10,11... | collective-permute-start | bytes 1105928 | tf_op jit(solution)/shard_map/ppermute | solution.py:407
  37.7 5.2 %copy-start = (s32[1,64,1]{1,2,0:T(1,128)S(1)}, s32[1,64,1]{1,2,0:T(1,128)}, u32[]{:S(2)}) copy-start(s32[1,64,1]{1,2,0:T(1,128)} %param.8) | copy-start | bytes 772
  37.7 2.4 %collective-permute-start.14 = (f32[2,40,768]{2,1,0:T(8,128)S(1)}, f32[2,40,768]{2,1,0:T(8,128)S(1)}, u32[]{:S(2)}, u32[]{:S(2)}) collective-permute-start(f32[2,40,768]{2,1,0:T(8,128)S(1)} %get-tuple-element.35.refs_0_), channel_id=1, source_target_pairs={{0,1},{1,0},{2,3},{3,2},{4,5},{5,4},{6,7},{7,6},{8,9},{9,8},{10,11... | collective-permute-start | bytes 737288 | tf_op jit(solution)/shard_map/ppermute | solution.py:407
  38.6 7.2 %collective-permute-start.19 = (bf16[72,896]{1,0:T(8,128)(2,1)S(1)}, bf16[72,896]{1,0:T(8,128)(2,1)S(1)}, u32[]{:S(2)}, u32[]{:S(2)}) collective-permute-start(bf16[72,896]{1,0:T(8,128)(2,1)S(1)} %get-tuple-element.41), channel_id=1, source_target_pairs={{0,2},{2,0},{4,6},{6,4},{8,10},{10,8},{12,14},{14,12},{1,3},{3,1},... | collective-permute-start | bytes 387080 | tf_op jit(solution)/shard_map/ppermute | solution.py:359
  40.1 7.1 %collective-permute-start.20 = (bf16[72,896]{1,0:T(8,128)(2,1)S(1)}, bf16[72,896]{1,0:T(8,128)(2,1)S(1)}, u32[]{:S(2)}, u32[]{:S(2)}) collective-permute-start(bf16[72,896]{1,0:T(8,128)(2,1)S(1)} %get-tuple-element.42), channel_id=1, source_target_pairs={{0,4},{2,6},{4,0},{6,2},{8,12},{10,14},{12,8},{14,10},{1,5},{3,7},... | collective-permute-start | bytes 387080 | tf_op jit(solution)/shard_map/ppermute | solution.py:359
  40.9 7.9 %collective-permute-start.21 = (bf16[72,896]{1,0:T(8,128)(2,1)S(1)}, bf16[72,896]{1,0:T(8,128)(2,1)S(1)}, u32[]{:S(2)}, u32[]{:S(2)}) collective-permute-start(bf16[72,896]{1,0:T(8,128)(2,1)S(1)} %get-tuple-element.43), channel_id=1, source_target_pairs={{0,6},{2,4},{4,2},{6,0},{8,14},{10,12},{12,10},{14,8},{1,7},{3,5},... | collective-permute-start | bytes 387080 | tf_op jit(solution)/shard_map/ppermute | solution.py:359
  42.9 7.1 %collective-permute-start = (s32[1,64]{1,0:T(1,128)S(1)}, s32[1,64]{1,0:T(1,128)S(1)}, u32[]{:S(2)}, u32[]{:S(2)}) collective-permute-start(s32[1,64]{1,0:T(1,128)S(1)} %bitcast.20), channel_id=1, source_target_pairs={{0,16},{16,0},{1,17},{17,1},{2,18},{18,2},{3,19},{19,3},{4,20},{20... | collective-permute-start | bytes 776 | tf_op jit(solution)/shard_map/ppermute | solution.py:378
  45.1 14.5 %collective-permute-start.4 = (bf16[72,896]{1,0:T(8,128)(2,1)S(1)}, bf16[72,896]{1,0:T(8,128)(2,1)S(1)}, u32[]{:S(2)}, u32[]{:S(2)}) collective-permute-start(bf16[72,896]{1,0:T(8,128)(2,1)S(1)} %get-tuple-element.30), channel_id=1, source_target_pairs={{0,16},{2,18},{4,20},{6,22},{8,24},{10,26},{12,28},{14,30},{16,0},... | collective-permute-start | bytes 387080 | tf_op jit(solution)/shard_map/ppermute | solution.py:376
  45.7 16.2 %collective-permute-start.5 = (bf16[72,896]{1,0:T(8,128)(2,1)S(1)}, bf16[72,896]{1,0:T(8,128)(2,1)S(1)}, u32[]{:S(2)}, u32[]{:S(2)}) collective-permute-start(bf16[72,896]{1,0:T(8,128)(2,1)S(1)} %get-tuple-element.31), channel_id=1, source_target_pairs={{0,16},{2,18},{4,20},{6,22},{8,24},{10,26},{12,28},{14,30},{16,2},... | collective-permute-start | bytes 387080 | tf_op jit(solution)/shard_map/ppermute | solution.py:376
  47.2 14.7 %collective-permute-start.6 = (bf16[72,896]{1,0:T(8,128)(2,1)S(1)}, bf16[72,896]{1,0:T(8,128)(2,1)S(1)}, u32[]{:S(2)}, u32[]{:S(2)}) collective-permute-start(bf16[72,896]{1,0:T(8,128)(2,1)S(1)} %get-tuple-element.32), channel_id=1, source_target_pairs={{0,16},{2,18},{4,20},{6,22},{8,24},{10,26},{12,28},{14,30},{16,4},... | collective-permute-start | bytes 387080 | tf_op jit(solution)/shard_map/ppermute | solution.py:376
  48.7 13.2 %collective-permute-start.15 = (bf16[72,896]{1,0:T(8,128)(2,1)S(1)}, bf16[72,896]{1,0:T(8,128)(2,1)S(1)}, u32[]{:S(2)}, u32[]{:S(2)}) collective-permute-start(bf16[72,896]{1,0:T(8,128)(2,1)S(1)} %get-tuple-element.36), channel_id=1, source_target_pairs={{0,16},{2,18},{4,20},{6,22},{8,24},{10,26},{12,28},{14,30},{16,6},... | collective-permute-start | bytes 387080 | tf_op jit(solution)/shard_map/ppermute | solution.py:376
  50.0 12.6 %collective-permute-start.22 = (bf16[72,896]{1,0:T(8,128)(2,1)S(1)}, bf16[72,896]{1,0:T(8,128)(2,1)S(1)}, u32[]{:S(2)}, u32[]{:S(2)}) collective-permute-start(bf16[72,896]{1,0:T(8,128)(2,1)S(1)} %add_convert_fusion), channel_id=1, source_target_pairs={{0,16},{2,18},{4,20},{6,22},{8,24},{10,26},{12,28},{14,30},{16,12}... | collective-permute-start | bytes 387080 | tf_op jit(solution)/shard_map/ppermute | solution.py:376
